TPU v7x, 8 devices: a whole 2x2x1 slice. The times are simulated.
8 devices in a mesh: rep: 1 (over z), data: 2 (over y), model: 4 (over x, core).
Axes of the slice: x: 2, y: 2, z: 1, core: 2. Of those that a mesh axis runs over, the one named last changes fastest.
Arguments:
- x_in: bfloat16 [16, 512, 4096], P(('rep', 'data'), 'model')
- key_lens: int32 [16], P(('rep', 'data'))
- ln_gain: bfloat16 [2, 4096], P(None, 'data')
- w_in: bfloat16 [2, 4096, 33792], P(None, 'data', 'model')
- w_out_attn: bfloat16 [2, 4096, 4096], P(None, 'model', 'data')
- w_out_mlp: bfloat16 [2, 14336, 4096], P(None, 'model', 'data')
Outputs:
- output: bfloat16 [16, 512, 4096], P(('rep', 'data'), 'model')
All inputs are finite; a program needn't handle non-finite values.
Results may differ from a plain program's by a relative error of at most 0.0162603.
Values are sent between devices in bfloat16 or wider.
A program may use at most 1 GiB of HBM per device.

v0:
```python
import jax
import jax.numpy as jnp
from jax import lax
from jax.sharding import PartitionSpec as P, NamedSharding

EPSILON = 1e-6


def layer_norm(act_in, gain_vec):
    act_f32 = act_in.astype(jnp.float32)
    row_mean = jnp.mean(act_f32, axis=-1, keepdims=True)
    centered = act_f32 - row_mean
    row_var = jnp.mean(centered * centered, axis=-1, keepdims=True)
    return (centered * lax.rsqrt(row_var + EPSILON) * gain_vec.astype(jnp.float32)).astype(jnp.bfloat16)


def solution(mesh):
    n_groups = mesh.shape['model']
    batch_axes = ('rep', 'data')

    def device_step(x_loc, len_loc, gain_loc, w_in_loc, w_attn_loc, w_mlp_loc):
        n_layers = w_in_loc.shape[0]
        block_in = w_in_loc.shape[2]
        attn_width = w_attn_loc.shape[1]
        ff_local = w_mlp_loc.shape[1]
        head_dim = (block_in - attn_width - 2 * ff_local) // 2
        q_group = attn_width // head_dim
        batch_loc, seq_loc = x_loc.shape[0], x_loc.shape[1]
        seq_len = seq_loc * n_groups
        kv_start = attn_width
        ff_start = attn_width + 2 * head_dim
        positions = jnp.arange(seq_len)
        allowed = (positions[None, :] <= positions[:, None])[None, :, :] & (positions[None, None, :] < len_loc[:, None, None])
        allowed = allowed[:, None, :, :]
        hidden = x_loc
        for layer_idx in range(n_layers):
            gain_full = lax.all_gather(gain_loc[layer_idx], 'data', axis=0, tiled=True)
            w_in_full = lax.all_gather(w_in_loc[layer_idx], 'data', axis=0, tiled=True)
            w_attn_full = lax.all_gather(w_attn_loc[layer_idx], 'data', axis=1, tiled=True)
            w_mlp_full = lax.all_gather(w_mlp_loc[layer_idx], 'data', axis=1, tiled=True)
            normed = layer_norm(hidden, gain_full)
            h_full = lax.all_gather(normed, 'model', axis=1, tiled=True)
            projected = jnp.dot(h_full, w_in_full, preferred_element_type=jnp.float32).astype(jnp.bfloat16)
            queries = projected[:, :, :attn_width].reshape(batch_loc, seq_len, q_group, head_dim)
            key_head = projected[:, :, kv_start:kv_start + head_dim]
            value_head = projected[:, :, kv_start + head_dim:ff_start]
            gate_proj = projected[:, :, ff_start:ff_start + ff_local]
            up_proj = projected[:, :, ff_start + ff_local:]
            scores = jnp.einsum('crke,cle->ckrl', queries, key_head, preferred_element_type=jnp.float32) * head_dim ** -0.5
            scores = jnp.where(allowed, scores, -1e30)
            soft_probs = jax.nn.softmax(scores, axis=-1)
            attn_heads = jnp.einsum('ckrl,cle->crke', soft_probs, value_head, preferred_element_type=jnp.float32).astype(jnp.bfloat16)
            attn_heads = attn_heads.reshape(batch_loc, seq_len, attn_width)
            mlp_act = (jax.nn.silu(gate_proj.astype(jnp.float32)) * up_proj.astype(jnp.float32)).astype(jnp.bfloat16)
            group_part = (jnp.dot(attn_heads, w_attn_full, preferred_element_type=jnp.float32) + jnp.dot(mlp_act, w_mlp_full, preferred_element_type=jnp.float32)).astype(jnp.bfloat16)
            z_loc = lax.psum_scatter(group_part, 'model', scatter_dimension=1, tiled=True)
            hidden = (hidden.astype(jnp.float32) + z_loc.astype(jnp.float32)).astype(jnp.bfloat16)
        return hidden

    return jax.shard_map(device_step, mesh=mesh, in_specs=(P(batch_axes, 'model', None), P(batch_axes), P(None, 'data'), P(None, 'data', 'model'), P(None, 'model', 'data'), P(None, 'model', 'data')), out_specs=P(batch_axes, 'model', None), check_vma=False)
```

profile of v0, /device:TPU:0, one launch (start us, length us, event | category | flops | bytes accessed | tf_op | source)
XLA Modules:
  0.0 3654.7 jit_solution(601981766465741822)
XLA Ops:
  6.5 1.4 fusion.80
  7.9 5.7 all-gather
  13.6 4.5 convert_reduce_fusion.1
  18.2 5.7 fusion.51
  23.9 11.5 fusion.53
  35.4 0.0 all-gather.21.cloned.1.call-start
  35.4 44.6 %fusion.77 = (bf16[1,2048,8448]{2,1,0:T(8,128)(2,1)}, bf16[1,2048,8448]{2,1,0:T(8,128)(2,1)}) fusion(bf16[2,2048,8448]{2,1,0:T(8,128)(2,1)} %param.9), kind=kLoop, calls=%fused_computation.95 | loop fusion | bytes 138412032 | tf_op jit(solution)/shard_map/slice | solution.py:38
  80.0 0.0 all-gather.25.cloned.1.call-start
  80.1 22.3 fusion.78
  102.4 0.0 all-gather.23.cloned.1.call-start
  102.5 6.1 fusion.79
  108.6 0.3 reduce-scatter.3.cloned.1.call-start
  108.8 0.1 iota_compare_fusion
  108.9 0.1 iota_compare_fusion.1
  109.0 2.1 broadcast_and_fusion
  111.1 125.3 %all-gather.17.cloned.1.call-done = bf16[8,512,4096]{2,1,0:T(8,128)(2,1)} async-done(((bf16[8,128,4096]{2,1,0:T(8,128)(2,1)}), bf16[8,512,4096]{2,1,0:T(8,128)(2,1)}) %all-gather.17.cloned.1.call-update) | async-done | bytes 33554448 | tf_op jit(solution)/shard_map/all_gather | solution.py:42
  236.4 790.0 %all-gather.21.cloned.1.call-done = bf16[1,4096,8448]{2,1,0:T(8,128)(2,1)} async-done(((bf16[1,2048,8448]{2,1,0:T(8,128)(2,1)}), bf16[1,4096,8448]{2,1,0:T(8,128)(2,1)}) %all-gather.21.cloned.1.call-update) | async-done | bytes 69206032 | tf_op jit(solution)/shard_map/all_gather | solution.py:38
  1026.4 314.4 %fusion.8 = bf16[8,512,8448]{2,1,0:T(8,128)(2,1)} fusion(bf16[8,512,4096]{2,1,0:T(8,128)(2,1)} %all-gather.17.cloned.1.call-done, bf16[1,4096,8448]{2,1,0:T(8,128)(2,1)} %all-gather.21.cloned.1.call-done), kind=kOutput, calls=%fused_computation.18 | convolution fusion | flops 283502444544 | bytes 171966464 | tf_op jit(solution)/shard_map/dot_general | solution.py:43
  1340.8 26.9 fusion.26
  1367.7 22.0 fusion.14
  1389.7 143.7 %fusion.40 = f32[8,512,4096]{2,1,0:T(8,128)} fusion(bf16[1,3584,4096]{2,1,0:T(8,128)(2,1)} %all-gather.25.cloned.1.call-done, bf16[8,512,8448]{2,1,0:T(8,128)(2,1)} %fusion.8), kind=kOutput, calls=%fused_computation.46 | convolution fusion | flops 120376524800 | bytes 155189248 | tf_op jit(solution)/shard_map/dot_general | solution.py:55
  1533.5 29.4 fusion.64
  1562.9 47.3 %add_convert_fusion.1 = bf16[8,512,4096]{2,1,0:T(8,128)(2,1)} fusion(f32[8,512,4096]{2,1,0:T(8,128)} %fusion.40, bf16[8,512,1024]{1,2,0:T(8,128)(2,1)} %bitcast.108, bf16[1,1024,4096]{2,1,0:T(8,128)(2,1)} %all-gather.23.cloned.1.call-done), kind=kOutput, calls=%fused_computation.12 | convolution fusion | flops 34393292800 | bytes 117440512 | tf_op jit(solution)/shard_map/dot_general | solution.py:55
  1610.2 0.0 all-gather.27.cloned.1.call-start
  1610.3 0.5 all-gather.27.cloned.1.call-update
  1610.8 0.0 all-gather.19.cloned.1.call-start
  1610.8 0.0 copy-done.11
  1610.9 4.3 all-gather.4
  1615.2 221.1 %reduce-scatter.3.cloned.1.call-done = bf16[8,128,4096]{2,1,0:T(8,128)(2,1)} async-done(((bf16[8,512,4096]{2,1,0:T(8,128)(2,1)}), bf16[8,128,4096]{2,1,0:T(8,128)(2,1)}) %reduce-scatter.3.cloned.1.call-update) | async-done | bytes 8388624 | tf_op jit(solution)/shard_map/reduce_scatter | solution.py:56
  1836.4 7.6 convert_reduce_fusion
  1844.0 3.4 copy-done
  1847.4 2.3 fusion.48
  1849.7 11.3 fusion.50
  1861.0 0.0 all-gather.31.cloned.1.call-start
  1861.0 0.7 all-gather.31.cloned.1.call-update
  1861.7 0.0 all-gather.29.cloned.1.call-start
  1861.8 0.7 all-gather.29.cloned.1.call-update
  1862.5 0.0 reduce-scatter.5.cloned.1.call-start
  1862.5 763.7 %all-gather.27.cloned.1.call-done = bf16[1,4096,8448]{2,1,0:T(8,128)(2,1)} async-done(((bf16[1,2048,8448]{2,1,0:T(8,128)(2,1)}), bf16[1,4096,8448]{2,1,0:T(8,128)(2,1)}) %all-gather.27.cloned.1.call-update) | async-done | bytes 69206032 | tf_op jit(solution)/shard_map/all_gather | solution.py:38
  2626.2 200.9 %all-gather.19.cloned.1.call-done = bf16[8,512,4096]{2,1,0:T(8,128)(2,1)} async-done(((bf16[8,128,4096]{2,1,0:T(8,128)(2,1)}), bf16[8,512,4096]{2,1,0:T(8,128)(2,1)}) %all-gather.19.cloned.1.call-update) | async-done | bytes 33554448 | tf_op jit(solution)/shard_map/all_gather | solution.py:42
  2827.2 314.6 %fusion.11 = bf16[8,512,8448]{2,1,0:T(8,128)(2,1)} fusion(bf16[8,512,4096]{2,1,0:T(8,128)(2,1)} %all-gather.19.cloned.1.call-done, bf16[1,4096,8448]{2,1,0:T(8,128)(2,1)} %all-gather.27.cloned.1.call-done), kind=kOutput, calls=%fused_computation.19 | convolution fusion | flops 283502444544 | bytes 171966464 | tf_op jit(solution)/shard_map/dot_general | solution.py:43
  3141.8 26.9 fusion.27
  3168.7 22.0 fusion.15
  3190.7 143.5 %fusion.38 = f32[8,512,4096]{2,1,0:T(8,128)} fusion(bf16[1,3584,4096]{2,1,0:T(8,128)(2,1)} %all-gather.31.cloned.1.call-done, bf16[8,512,8448]{2,1,0:T(8,128)(2,1)} %fusion.11), kind=kOutput, calls=%fused_computation.44 | convolution fusion | flops 120376524800 | bytes 155189248 | tf_op jit(solution)/shard_map/dot_general | solution.py:55
  3334.2 29.5 fusion.67
  3363.7 47.4 %add_convert_fusion = bf16[8,512,4096]{2,1,0:T(8,128)(2,1)} fusion(f32[8,512,4096]{2,1,0:T(8,128)} %fusion.38, bf16[8,512,1024]{1,2,0:T(8,128)(2,1)} %bitcast.107, bf16[1,1024,4096]{2,1,0:T(8,128)(2,1)} %all-gather.29.cloned.1.call-done), kind=kOutput, calls=%fused_computation.10 | convolution fusion | flops 34393292800 | bytes 117440512 | tf_op jit(solution)/shard_map/dot_general | solution.py:55
  3411.1 226.2 %reduce-scatter.5.cloned.1.call-done = bf16[8,128,4096]{2,1,0:T(8,128)(2,1)} async-done(((bf16[8,512,4096]{2,1,0:T(8,128)(2,1)}), bf16[8,128,4096]{2,1,0:T(8,128)(2,1)}) %reduce-scatter.5.cloned.1.call-update) | async-done | bytes 8388624 | tf_op jit(solution)/shard_map/reduce_scatter | solution.py:56
  3637.3 10.1 fusion.55
  (42 shorter events, 0.2 us)
Async XLA Ops:
  6.5 229.8 %all-gather.17.cloned.1.call-start = ((), (), s32[]{:S(2)}) async-start(), calls=%async_computation.2 | async-start | bytes 41943040 | tf_op jit(solution)/shard_map/all_gather | solution.py:42
  35.4 991.0 %all-gather.21.cloned.1.call-start = ((), (), s32[]{:S(2)}) async-start(), calls=%async_computation.6 | async-start | bytes 103809024 | tf_op jit(solution)/shard_map/all_gather | solution.py:38
  80.0 28.9 copy-start.12
  80.0 1309.7 %all-gather.25.cloned.1.call-start = ((), (), s32[]{:S(2)}) async-start(), calls=%async_computation.8 | async-start | bytes 44040192 | tf_op jit(solution)/shard_map/all_gather | solution.py:40
  102.4 1460.5 %all-gather.23.cloned.1.call-start = ((), (), s32[]{:S(2)}) async-start(), calls=%async_computation.7 | async-start | bytes 12582912 | tf_op jit(solution)/shard_map/all_gather | solution.py:39
  108.6 1727.8 %reduce-scatter.3.cloned.1.call-start = ((), (), s32[]{:S(2)}) async-start(), calls=%async_computation.3 | async-start | bytes 41943040 | tf_op jit(solution)/shard_map/reduce_scatter | solution.py:56
  1026.4 314.5 %copy-start.1 = (pred[8,512,512]{1,2,0:T(8,128)(4,1)S(1)}, pred[8,512,512]{1,2,0:T(8,128)(4,1)}, u32[]{:S(2)}) copy-start(pred[8,512,512]{1,2,0:T(8,128)(4,1)} %broadcast_and_fusion) | copy-start | bytes 6291460
  1367.7 22.0 copy-start.7
  1389.7 143.8 %copy-start.2 = (pred[8,512,512]{1,2,0:T(8,128)(4,1)S(1)}, pred[8,512,512]{1,2,0:T(8,128)(4,1)}, u32[]{:S(2)}) copy-start(pred[8,512,512]{1,2,0:T(8,128)(4,1)} %broadcast_and_fusion) | copy-start | bytes 6291460
  1389.7 143.8 %copy-start.8 = (f32[8,8,512]{2,1,0:T(8,128)S(1)}, f32[8,8,512]{2,1,0:T(8,128)}, u32[]{:S(2)}) copy-start(f32[8,8,512]{2,1,0:T(8,128)} %copy-done.7) | copy-start | bytes 393220
  1389.7 143.8 %copy-start.10 = (f32[8,8,512]{2,1,0:T(8,128)S(1)}, f32[8,8,512]{2,1,0:T(8,128)}, u32[]{:S(2)}) copy-start(f32[8,8,512]{2,1,0:T(8,128)} %fusion.14) | copy-start | bytes 393220
  1610.2 0.7 copy-start.11
  1610.2 1016.0 %all-gather.27.cloned.1.call-start = ((), (), s32[]{:S(2)}) async-start(), calls=%async_computation.9 | async-start | bytes 103809024 | tf_op jit(solution)/shard_map/all_gather | solution.py:38
  1610.8 1216.4 %all-gather.19.cloned.1.call-start = ((), (), s32[]{:S(2)}) async-start(), calls=%async_computation.4 | async-start | bytes 41943040 | tf_op jit(solution)/shard_map/all_gather | solution.py:42
  1844.0 3.4 copy-start
  1861.0 1329.7 %all-gather.31.cloned.1.call-start = ((), (), s32[]{:S(2)}) async-start(), calls=%async_computation.11 | async-start | bytes 44040192 | tf_op jit(solution)/shard_map/all_gather | solution.py:40
  1861.7 1502.0 %all-gather.29.cloned.1.call-start = ((), (), s32[]{:S(2)}) async-start(), calls=%async_computation.10 | async-start | bytes 12582912 | tf_op jit(solution)/shard_map/all_gather | solution.py:39
  1862.5 1774.8 %reduce-scatter.5.cloned.1.call-start = ((), (), s32[]{:S(2)}) async-start(), calls=%async_computation.5 | async-start | bytes 41943040 | tf_op jit(solution)/shard_map/reduce_scatter | solution.py:56
  2827.2 314.6 %copy-start.3 = (pred[8,512,512]{1,2,0:T(8,128)(4,1)S(1)}, pred[8,512,512]{1,2,0:T(8,128)(4,1)}, u32[]{:S(2)}) copy-start(pred[8,512,512]{1,2,0:T(8,128)(4,1)} %broadcast_and_fusion) | copy-start | bytes 6291460
  3168.7 22.0 copy-start.5
  3190.7 143.5 %copy-start.4 = (pred[8,512,512]{1,2,0:T(8,128)(4,1)S(1)}, pred[8,512,512]{1,2,0:T(8,128)(4,1)}, u32[]{:S(2)}) copy-start(pred[8,512,512]{1,2,0:T(8,128)(4,1)} %broadcast_and_fusion) | copy-start | bytes 6291460
  3190.7 143.5 %copy-start.6 = (f32[8,8,512]{2,1,0:T(8,128)S(1)}, f32[8,8,512]{2,1,0:T(8,128)}, u32[]{:S(2)}) copy-start(f32[8,8,512]{2,1,0:T(8,128)} %copy-done.5) | copy-start | bytes 393220
  3190.7 143.5 %copy-start.9 = (f32[8,8,512]{2,1,0:T(8,128)S(1)}, f32[8,8,512]{2,1,0:T(8,128)}, u32[]{:S(2)}) copy-start(f32[8,8,512]{2,1,0:T(8,128)} %fusion.15) | copy-start | bytes 393220
Sparse Core Ops, SparseCore 0:
  35.5 200.8 all-gather.16
  237.9 788.4 all-gather.20
  1027.9 339.3 all-gather.24
  1368.7 102.2 all-gather.22
  1610.3 225.9 reduce-scatter.2
  1837.8 788.4 all-gather.26
  2627.8 199.3 all-gather.18
  2828.7 339.3 all-gather.30
  3169.6 102.2 all-gather.28
  3411.2 225.9 reduce-scatter.4
where the time goes:
time: 3660 us; the launch traced here: 3650 us
  waiting for transfers between devices  2330 us (64%)
  matrix products  1120 us (31%)
  other arithmetic  99.3 us (3%)
  local copies, waits for them, and re-layouts  77.8 us (2%)
    all_gather x2, waiting for transfers between devices, device_step(): w_in_full = lax.all_gather(w_in_loc[layer_idx], 'data', axis=0, tiled=True)  1550 us
    dot_general x2, matrix products, device_step(): jnp.dot(h_full, w_in_full, preferred_element_type=jnp.float32)  629 us
    reduce_scatter x2, waiting for transfers between devices, device_step(): lax.psum_scatter(group_part, 'model', scatter_dimension=1, tiled=True)  447 us
    all_gather x2, waiting for transfers between devices, device_step(): h_full = lax.all_gather(normed, 'model', axis=1, tiled=True)  326 us
    dot_general x2, matrix products, device_step(): jnp.dot(mlp_act, w_mlp_full, preferred_element_type=jnp.float32)  287 us
    dot_general x2, matrix products, device_step(): jnp.dot(attn_heads, w_attn_full, preferred_element_type=jnp.float32)  94.7 us
  transfers between devices with their start and end apart: 10, of which 6 were waited for; matrix products, arithmetic and copies ran while one was open for 32% of the time, Pallas kernels for 0%

commit v1 on v0

v1 whole, which is shorter than its diff:
```python
import jax
import jax.numpy as jnp
from jax import lax
from jax.experimental import pallas as pl
from jax.experimental.pallas import tpu as pltpu
from jax.sharding import PartitionSpec as P

EPSILON = 1e-6
HEAD = 128
UNIT = 256
TILE = 512
NEG = -1e30
MESH = pl.DeviceIdType.MESH
BF = jnp.bfloat16
F32 = jnp.float32


def make_kernel(rows, seqs, d, dh, block_in, aw, ff, n_units):
    q_heads = aw // HEAD
    ff0 = aw + 2 * HEAD
    n_gu = ff // UNIT
    gate_u = ff0 // UNIT
    up_u = (ff0 + ff) // UNIT
    kv_u = aw // UNIT
    n_q = aw // TILE
    n_out = d // TILE
    n_half = n_out // 2
    pos = rows // seqs
    early = 8
    visits = 2 * early + (n_gu - early)
    kk = aw + ff
    lnr = 64
    n_ln = rows // lnr
    n_hb = n_ln // 2
    hb = 2 * lnr
    qscale = HEAD ** -0.5 * 1.4426950408889634

    def kernel(x, lens, gain, w_in, w_at, w_ml,
               y_out, a_in, a_at, a_ml, r_in, r_at, r_ml, h_all, kvb, q_b, m_b, z_b, xr, yq, yr, hid,
               big, wv, ov, xin, hst, gv, lv, qv, kvv,
               a_s, a_r, wy_s, wy_r, wc_s, wc_r, oy_s, oy_r, oc_s, oc_r, hy_s, hy_r, hx_s, hx_r, hf_s, hf_r,
               kv_s, kv_r, xz_s, xz_r, yz_s, yz_r, g_s, g_r, lg, li, lh, lo, hl, ws, os_, ai, ml_s, ad):
        rep = lax.axis_index('rep')
        y = lax.axis_index('data')
        m = lax.axis_index('model')
        xx = lax.div(m, 2)
        c = lax.rem(m, 2)
        ypeer = (rep, 1 - y, m)
        xpeer = (rep, y, lax.rem(m + 2, 4))
        cpeer = (rep, y, m + 1 - 2 * c)
        keeper = c == y
        giver = c != y

        def remote(src, dst, ss, rs, dev):
            return pltpu.make_async_remote_copy(src_ref=src, dst_ref=dst, send_sem=ss, recv_sem=rs, device_id=dev,
                                                device_id_type=MESH)

        def local(src, dst, sem):
            return pltpu.make_async_copy(src, dst, sem)

        def loop(lo_, hi_, body):
            def step(i, carry):
                body(i)
                return carry
            lax.fori_loop(lo_, hi_, step, 0)

        def ucols(u):
            return pl.ds(pl.multiple_of(u * UNIT, UNIT), UNIT)

        def tcols(t):
            return pl.ds(pl.multiple_of(t * TILE, TILE), TILE)

        def wy(l, u):
            return remote(w_in.at[l, :, ucols(u)], r_in.at[l, :, ucols(u)], wy_s.at[l, u], wy_r.at[l, u], ypeer)

        def wc(l, u):
            return remote(r_in.at[l, :, ucols(u)], r_in.at[l, :, ucols(u)], wc_s.at[l, u], wc_r.at[l, u], cpeer)

        def oy(l, t):
            return (remote(w_at.at[l, :, tcols(t)], r_at.at[l, :, tcols(t)], oy_s.at[l, t, 0], oy_r.at[l, t, 0], ypeer),
                    remote(w_ml.at[l, :, tcols(t)], r_ml.at[l, :, tcols(t)], oy_s.at[l, t, 1], oy_r.at[l, t, 1], ypeer))

        def oc(l, t):
            return (remote(r_at.at[l, :, tcols(t)], r_at.at[l, :, tcols(t)], oc_s.at[l, t, 0], oc_r.at[l, t, 0], cpeer),
                    remote(r_ml.at[l, :, tcols(t)], r_ml.at[l, :, tcols(t)], oc_s.at[l, t, 1], oc_r.at[l, t, 1], cpeer))

        def acopy(l):
            return (remote(w_in.at[l], a_in.at[l], a_s.at[l, 0], a_r.at[l, 0], cpeer),
                    remote(w_at.at[l], a_at.at[l], a_s.at[l, 1], a_r.at[l, 1], cpeer),
                    remote(w_ml.at[l], a_ml.at[l], a_s.at[l, 2], a_r.at[l, 2], cpeer))

        def hrows(b):
            return pl.ds(pl.multiple_of(b * hb, hb), hb)

        def hy(l, b):
            return remote(h_all.at[l, 0, hrows(b)], h_all.at[l, 1, hrows(b)], hy_s.at[l, b], hy_r.at[l, b], ypeer)

        def hx(l, b):
            return remote(h_all.at[l, 0, hrows(b)], h_all.at[l, 2, hrows(b)], hx_s.at[l, b], hx_r.at[l, b], xpeer)

        def hf(l):
            return remote(h_all.at[l, 1], h_all.at[l, 3], hf_s.at[l], hf_r.at[l], xpeer)

        def kvx(l):
            return remote(kvb.at[l, 0], kvb.at[l, 1], kv_s.at[l], kv_r.at[l], cpeer)

        def xz(l, t, i):
            return remote(z_b.at[l, 2 + i, :, tcols(t)], xr.at[l, i, :, tcols(t)], xz_s.at[l, t, i], xz_r.at[l, t, i], xpeer)

        def yz(l, t):
            return remote(yq.at[l, :, tcols(t)], yr.at[l, :, tcols(t)], yz_s.at[l, t], yz_r.at[l, t], ypeer)

        def issue_gu(l, j):
            wy(l, gate_u + j).start()
            wy(l, up_u + j).start()

        def issue_qkv(l):
            wy(l, kv_u).start()
            loop(0, kv_u, lambda u: wy(l, u).start())

        def issue_o(l, t):
            for cp in oy(l, t):
                cp.start()

        def arrive(l, u):
            @pl.when(keeper)
            def _():
                wy(l, u).wait_recv()
                wc(l, u).start()

            @pl.when(giver)
            def _():
                wc(l, u).wait_recv()

        def arrive_o(l, t):
            @pl.when(keeper)
            def _():
                for cp, fw in zip(oy(l, t), oc(l, t)):
                    cp.wait_recv()
                    fw.start()

            @pl.when(giver)
            def _():
                for fw in oc(l, t):
                    fw.wait_recv()

        def near_in(l, u, slot, half):
            return wv.at[slot, pl.ds(pl.multiple_of(y * dh, dh), dh), half * UNIT:(half + 1) * UNIT]

        def load_unit(l, u, slot, half):
            near = wv.at[slot, pl.ds(pl.multiple_of(y * dh, dh), dh), half * UNIT:(half + 1) * UNIT]
            far = wv.at[slot, pl.ds(pl.multiple_of((1 - y) * dh, dh), dh), half * UNIT:(half + 1) * UNIT]

            @pl.when(keeper)
            def _():
                local(w_in.at[l, :, ucols(u)], near, ws.at[slot, half]).start()

            @pl.when(giver)
            def _():
                local(a_in.at[l, :, ucols(u)], near, ws.at[slot, half]).start()

            local(r_in.at[l, :, ucols(u)], far, ws.at[slot, 2 + half]).start()

        def wait_unit(slot, half):
            near = wv.at[slot, pl.ds(pl.multiple_of(y * dh, dh), dh), half * UNIT:(half + 1) * UNIT]
            far = wv.at[slot, pl.ds(pl.multiple_of((1 - y) * dh, dh), dh), half * UNIT:(half + 1) * UNIT]
            local(r_in.at[0, :, ucols(0)], near, ws.at[slot, half]).wait()
            local(r_in.at[0, :, ucols(0)], far, ws.at[slot, 2 + half]).wait()

        def load_o(l, src_at, src_ml, t, slot):
            local(src_at.at[l, :, tcols(t)], wv.at[slot, 0:aw], ws.at[slot, 0]).start()
            local(src_ml.at[l, :, tcols(t)], wv.at[slot, aw:kk], ws.at[slot, 1]).start()

        def load_o_near(l, t, slot):
            @pl.when(keeper)
            def _():
                load_o(l, w_at, w_ml, t, slot)

            @pl.when(giver)
            def _():
                load_o(l, a_at, a_ml, t, slot)

        def wait_o(slot):
            local(r_at.at[0, :, tcols(0)], wv.at[slot, 0:aw], ws.at[slot, 0]).wait()
            local(r_ml.at[0, :, tcols(0)], wv.at[slot, aw:kk], ws.at[slot, 1]).wait()

        def lrows(r):
            return pl.ds(pl.multiple_of(r * lnr, lnr), lnr)

        def ln_phase(kind):
            l = 0 if kind == 0 else kind - 1
            ln = 1 if kind == 1 else 0
            base = hid if kind == 2 else x
            srcs = [base] if kind == 0 else [base, z_b.at[l, 0], xr.at[l, 0], yr.at[l]]

            def loads(r, slot):
                return [local(s.at[lrows(r)], xin.at[slot, i], li.at[slot, i]) for i, s in enumerate(srcs)]

            def store_h(r, slot):
                return local(big.at[0, lrows(r), 0:d], h_all.at[ln, 0, lrows(r)], lh.at[slot])

            def store_o(r, slot):
                return local(hst.at[slot], (hid if kind == 1 else y_out).at[lrows(r)], lo.at[slot])

            def send(b):
                hy(ln, b).start()
                hx(ln, b).start()

            for cp in loads(0, 0):
                cp.start()

            def block(r):
                slot = lax.rem(r, 2)

                @pl.when(r + 1 < n_ln)
                def _():
                    for cp in loads(r + 1, 1 - slot):
                        cp.start()
                for cp in loads(r, slot):
                    cp.wait()
                if kind > 0:
                    @pl.when(r >= 2)
                    def _():
                        store_o(r - 2, slot).wait()

                def sub(i):
                    rs = pl.ds(pl.multiple_of(i * 32, 32), 32)
                    v = xin[slot, 0, rs, :].astype(F32)
                    if kind > 0:
                        zs = xin[slot, 1, rs, :].astype(F32) + xin[slot, 2, rs, :].astype(F32)
                        v = (v + (zs + xin[slot, 3, rs, :].astype(F32))).astype(BF)
                        hst[slot, rs, :] = v
                        v = v.astype(F32)
                    if kind < 2:
                        mean = jnp.sum(v, axis=-1, keepdims=True) * (1.0 / d)
                        cen = v - mean
                        var = jnp.sum(cen * cen, axis=-1, keepdims=True) * (1.0 / d)
                        out = cen * lax.rsqrt(var + EPSILON) * gv[ln, 0:1, :]
                        big[0, pl.ds(pl.multiple_of(r * lnr + i * 32, 32), 32), 0:d] = out.astype(BF)
                loop(0, lnr // 32, sub)
                if kind > 0:
                    store_o(r, slot).start()
                if kind < 2:
                    store_h(r, slot).start()

                    @pl.when(r >= 1)
                    def _():
                        store_h(r - 1, 1 - slot).wait()

                    @pl.when(jnp.logical_and(r >= 2, lax.rem(r, 2) == 0))
                    def _():
                        send(lax.div(r, 2) - 1)
            loop(0, n_ln, block)
            if kind > 0:
                store_o(n_ln - 2, 0).wait()
                store_o(n_ln - 1, 1).wait()
            if kind < 2:
                store_h(n_ln - 1, 1).wait()
                send(n_hb - 1)

        barrier = pltpu.get_barrier_semaphore()
        for dev in (ypeer, xpeer, cpeer):
            pl.semaphore_signal(barrier, inc=1, device_id=dev, device_id_type=MESH)
        pl.semaphore_wait(barrier, 3)

        def gain_y():
            half = gv.at[:, :, pl.ds(pl.multiple_of(y * dh, dh), dh)]
            return remote(gain, half, g_s.at[0], g_r.at[0], ypeer)

        def lens_y():
            return remote(lens, lv.at[1], g_s.at[1], g_r.at[1], ypeer)

        def gain_l():
            return local(gain, gv.at[:, :, pl.ds(pl.multiple_of(y * dh, dh), dh)], lg.at[0])

        def lens_l():
            return local(lens, lv.at[0], lg.at[1])

        gain_y().start()
        lens_y().start()
        gain_l().start()
        lens_l().start()

        @pl.when(keeper)
        def _():
            for l in range(2):
                for cp in acopy(l):
                    cp.start()

        @pl.when(giver)
        def _():
            issue_gu(0, 0)
        gain_l().wait()
        lens_l().wait()
        gain_y().wait()
        lens_y().wait()
        ln_phase(0)

        @pl.when(giver)
        def _():
            loop(1, n_gu, lambda j: issue_gu(0, j))
            issue_qkv(0)
            loop(0, n_half, lambda t: issue_o(0, t))

        def layer(l):
            @pl.when(giver)
            def _():
                for cp in acopy(l):
                    cp.wait_recv()

            def h_load(s):
                return local(h_all.at[l, s], big.at[s, :, 0:d], hl.at[s])

            loop(0, n_hb, lambda b: hy(l, b).wait_recv())
            hf(l).start()
            h_load(1).start()
            loop(0, n_hb, lambda b: hx(l, b).wait_recv())
            h_load(2).start()
            arrive(l, gate_u)
            arrive(l, up_u)
            load_unit(l, gate_u, 0, 0)
            load_unit(l, up_u, 0, 1)
            h_load(1).wait()
            h_load(2).wait()

            def m_store(s, j):
                return local(ov.at[s, :, 0:UNIT], m_b.at[s, :, ucols(j)], os_.at[s])

            def visit(v):
                slot = lax.rem(v, 2)
                wait_unit(slot, 0)
                wait_unit(slot, 1)
                blk = lax.div(v, early)
                j = v - early * lax.div(lax.min(blk, 2) + 1, 2)
                s_lo = 3 * lax.rem(lax.min(blk, 2), 2)
                s_hi = 3 + lax.div(lax.min(blk, 2) + 1, 2)
                s_pf = s_lo + lax.div(s_hi - s_lo, 2)

                @pl.when(v == early)
                def _():
                    hf(l).wait_recv()
                    h_load(3).start()
                    h_load(3).wait()

                def shard(s):
                    @pl.when(s == s_pf)
                    def _():
                        nv = v + 1
                        nj = nv - early * lax.div(lax.min(lax.div(nv, early), 2) + 1, 2)

                        @pl.when(jnp.logical_and(lax.div(nv, early) != 1, nv < visits))
                        def _():
                            arrive(l, gate_u + nj)
                            arrive(l, up_u + nj)

                        @pl.when(nv < visits)
                        def _():
                            load_unit(l, gate_u + nj, 1 - slot, 0)
                            load_unit(l, up_u + nj, 1 - slot, 1)

                        @pl.when(nv == visits)
                        def _():
                            arrive(l, kv_u)
                            load_unit(l, kv_u, visits % 2, 0)

                    @pl.when(v != early * lax.div(s, 3))
                    def _():
                        m_store(s, 0).wait()
                    acc = jnp.dot(big[s, :, 0:d], wv[slot, 0:d, :], preferred_element_type=F32)
                    g = acc[:, :UNIT].astype(BF).astype(F32)
                    u = acc[:, UNIT:].astype(BF).astype(F32)
                    ov[s, :, 0:UNIT] = (g * jax.nn.sigmoid(g) * u).astype(BF)
                    m_store(s, j).start()
                loop(s_lo, s_hi, shard)
            loop(0, visits, visit)

            kslot = visits % 2
            wait_unit(kslot, 0)

            def kv_store(s):
                return local(ov.at[s, :, 0:UNIT], kvb.at[l, 0, s], os_.at[s])

            def kv_shard(s):
                @pl.when(s == 2)
                def _():
                    for u in range(2):
                        arrive(l, u)
                        load_unit(l, u, 1 - kslot, u)
                m_store(s, 0).wait()
                acc = jnp.dot(big[s, :, 0:d], wv[kslot, 0:d, 0:UNIT], preferred_element_type=F32)
                ov[s, :, 0:UNIT] = acc.astype(BF)
                kv_store(s).start()
            loop(0, 4, kv_shard)

            def q_store(s, t):
                return local(ov.at[s], q_b.at[s, :, tcols(t)], os_.at[s])

            def q_tile(t):
                slot = lax.rem(t + 1 - kslot, 2)
                wait_unit(slot, 0)
                wait_unit(slot, 1)

                def shard(s):
                    @pl.when(jnp.logical_and(s == 2, t + 1 < n_q))
                    def _():
                        for i in range(2):
                            arrive(l, 2 * (t + 1) + i)
                            load_unit(l, 2 * (t + 1) + i, 1 - slot, i)

                    @pl.when(t == 0)
                    def _():
                        kv_store(s).wait()

                    @pl.when(t > 0)
                    def _():
                        q_store(s, 0).wait()
                    acc = jnp.dot(big[s, :, 0:d], wv[slot, 0:d, :], preferred_element_type=F32)
                    ov[s] = acc.astype(BF)
                    q_store(s, t).start()
                loop(0, 4, shard)

                @pl.when(t == 0)
                def _():
                    kvx(l).start()
            loop(0, n_q, q_tile)
            loop(0, 4, lambda s: q_store(s, 0).wait())

            def m_load(s):
                return local(m_b.at[s], big.at[s, :, aw:kk], ml_s.at[s])
            loop(0, 4, lambda s: m_load(s).start())
            oslot = (1 - kslot + n_q) % 2
            load_o_near(l, 0, oslot)
            kvx(l).wait_recv()

            def at_loads(i, slot):
                a = lax.div(i, seqs)
                b = lax.rem(i, seqs)
                rs = pl.ds(pl.multiple_of(b * pos, pos), pos)

                def at(quarter):
                    return kvv.at[slot, pl.ds(pl.multiple_of(quarter * pos, pos), pos)]
                return (local(q_b.at[a, rs], qv.at[slot, xx], ai.at[slot, 0]),
                        local(q_b.at[2 + a, rs], qv.at[slot, 1 - xx], ai.at[slot, 1]),
                        local(kvb.at[l, 0, a, rs], at(2 * xx + c), ai.at[slot, 2]),
                        local(kvb.at[l, 0, 2 + a, rs], at(2 * (1 - xx) + c), ai.at[slot, 3]),
                        local(kvb.at[l, 1, a, rs], at(2 * xx + 1 - c), ai.at[slot, 4]),
                        local(kvb.at[l, 1, 2 + a, rs], at(2 * (1 - xx) + 1 - c), ai.at[slot, 5]))

            for cp in at_loads(0, 0):
                cp.start()

            def seq(i):
                slot = lax.rem(i, 2)
                a = lax.div(i, seqs)
                b = lax.rem(i, seqs)

                @pl.when(i + 1 < 2 * seqs)
                def _():
                    for cp in at_loads(i + 1, 1 - slot):
                        cp.start()
                for cp in at_loads(i, slot):
                    cp.wait()
                row = pl.ds(pl.multiple_of(b * pos, pos), pos)
                for blk in range(2):
                    nk = 2 * pos * (blk + 1)
                    qpos = lax.broadcasted_iota(jnp.int32, (pos, nk), 0) + (2 * blk + c) * pos
                    kpos = lax.broadcasted_iota(jnp.int32, (pos, nk), 1)
                    ok = jnp.logical_and(kpos <= qpos, kpos < lv[a, pl.ds(b, 1), 0:nk])
                    keys = kvv[slot, 0:nk, 0:HEAD]
                    vals = kvv[slot, 0:nk, HEAD:2 * HEAD]
                    sh = a + 2 * (blk + xx - 2 * blk * xx)
                    for hd in range(q_heads):
                        cs = slice(hd * HEAD, (hd + 1) * HEAD)
                        s = lax.dot_general(qv[slot, blk, :, cs], keys, (((1,), (1,)), ((), ())),
                                            preferred_element_type=F32) * qscale
                        s = jnp.where(ok, s, NEG)
                        e = jnp.exp2(s - jnp.max(s, axis=-1, keepdims=True))
                        den = jnp.sum(e, axis=-1, keepdims=True)
                        o = jnp.dot(e.astype(BF), vals, preferred_element_type=F32)
                        big[sh, row, cs] = (o / den).astype(BF)
            loop(0, 2 * seqs, seq)

            @pl.when(jnp.logical_and(giver, l == 0))
            def _():
                loop(0, 2, lambda j: issue_gu(1, j))
            loop(0, 4, lambda s: m_load(s).wait())

            def tau(k):
                return lax.rem(y + lax.div(k, n_half), 2) * n_half + lax.rem(k, n_half)

            def z_store(s, t):
                return local(ov.at[s], z_b.at[l, s, :, tcols(t)], os_.at[s])

            def out_tile(k):
                slot = lax.rem(k + oslot, 2)
                t = tau(k)
                wait_o(slot)

                def shard(si):
                    s = lax.rem(si + 2, 4)

                    @pl.when(jnp.logical_and(si == 2, k + 1 < n_half))
                    def _():
                        load_o_near(l, k + 1, 1 - slot)

                    @pl.when(jnp.logical_and(si == 2, jnp.logical_and(k + 1 >= n_half, k + 1 < n_out)))
                    def _():
                        arrive_o(l, k + 1 - n_half)
                        load_o(l, r_at, r_ml, k + 1 - n_half, 1 - slot)

                    @pl.when(jnp.logical_and(si >= 2, k > 0))
                    def _():
                        z_store(s, t).wait()

                    @pl.when(jnp.logical_and(si >= 1, si < 3))
                    def _():
                        z_store(si + 1, t).wait()
                        xz(l, t, si - 1).start()
                    acc = jnp.dot(big[s], wv[slot], preferred_element_type=F32)
                    ov[s] = acc.astype(BF)
                    z_store(s, t).start()
                loop(0, 4, shard)
            loop(0, n_out, out_tile)
            loop(0, 2, lambda s: z_store(s, 0).wait())

            def add_tile(k):
                t = tau(k)
                xz(l, t, 0).wait_recv()
                xz(l, t, 1).wait_recv()
                lhs = local(z_b.at[l, 1, :, tcols(t)], ov.at[0], ad.at[0])
                rhs = local(xr.at[l, 1, :, tcols(t)], ov.at[1], ad.at[1])
                lhs.start()
                rhs.start()
                lhs.wait()
                rhs.wait()

                def sub(i):
                    rs = pl.ds(pl.multiple_of(i * 128, 128), 128)
                    ov[0, rs, :] = (ov[0, rs, :].astype(F32) + ov[1, rs, :].astype(F32)).astype(BF)
                loop(0, rows // 128, sub)
                out = local(ov.at[0], yq.at[l, :, tcols(t)], ad.at[2])
                out.start()
                out.wait()
                yz(l, t).start()

                @pl.when(jnp.logical_and(giver, jnp.logical_and(l == 0, k >= 5)))
                def _():
                    issue_gu(1, k - 3)
            loop(0, n_out, add_tile)
            loop(0, n_out, lambda t: yz(l, t).wait_recv())

            @pl.when(l == 0)
            def _():
                ln_phase(1)

                @pl.when(giver)
                def _():
                    loop(5, n_gu, lambda j: issue_gu(1, j))
                    issue_qkv(1)
                    loop(0, n_half, lambda t: issue_o(1, t))

            @pl.when(l == 1)
            def _():
                ln_phase(2)

            def sent_h(b):
                hy(l, b).wait_send()
                hx(l, b).wait_send()
            loop(0, n_hb, sent_h)
            hf(l).wait_send()
            kvx(l).wait_send()

            def sent_z(t):
                xz(l, t, 0).wait_send()
                xz(l, t, 1).wait_send()
                yz(l, t).wait_send()
            loop(0, n_out, sent_z)

            @pl.when(giver)
            def _():
                loop(0, n_units, lambda u: wy(l, u).wait_send())

                def sent_o(t):
                    for cp in oy(l, t):
                        cp.wait_send()
                loop(0, n_half, sent_o)

            @pl.when(keeper)
            def _():
                loop(0, n_units, lambda u: wc(l, u).wait_send())

                def sent_o(t):
                    for cp in oc(l, t):
                        cp.wait_send()
                loop(0, n_half, sent_o)
                for cp in acopy(l):
                    cp.wait_send()
        loop(0, 2, layer)

    return kernel


def solution(mesh):
    batch_axes = ('rep', 'data')

    def device_step(x_loc, len_loc, gain_loc, w_in_loc, w_attn_loc, w_mlp_loc):
        seqs, pos, d = x_loc.shape
        rows = seqs * pos
        layers, dh, block_in = w_in_loc.shape
        aw = w_attn_loc.shape[1]
        ff = w_mlp_loc.shape[1]
        n_units = block_in // UNIT
        n_out = d // TILE
        kk = aw + ff
        seq_len = pos * mesh.shape['model']
        lens = jnp.broadcast_to(len_loc[:, None], (seqs, seq_len)).astype(jnp.int32)
        gain = jnp.broadcast_to(gain_loc.astype(F32)[:, None, :], (layers, 8, dh))

        def buf(*shape):
            return jax.ShapeDtypeStruct(shape, BF)

        outs = [buf(rows, d), buf(layers, dh, block_in), buf(layers, aw, dh), buf(layers, ff, dh),
                buf(layers, dh, block_in), buf(layers, aw, dh), buf(layers, ff, dh),
                buf(layers, 4, rows, d), buf(layers, 2, 4, rows, 2 * HEAD), buf(4, rows, aw), buf(4, rows, ff),
                buf(layers, 4, rows, d), buf(layers, 2, rows, d), buf(layers, rows, d), buf(layers, rows, d), buf(rows, d)]
        dma = pltpu.SemaphoreType.DMA
        n_hb = rows // 128
        scratch = [pltpu.VMEM((4, rows, kk), BF), pltpu.VMEM((2, kk, TILE), BF), pltpu.VMEM((4, rows, TILE), BF),
                   pltpu.VMEM((2, 4, 64, d), BF), pltpu.VMEM((2, 64, d), BF), pltpu.VMEM((layers, 8, d), F32),
                   pltpu.VMEM((2, seqs, seq_len), jnp.int32), pltpu.VMEM((2, 2, pos, aw), BF),
                   pltpu.VMEM((2, seq_len, 2 * HEAD), BF),
                   dma((layers, 3)), dma((layers, 3)),
                   dma((layers, n_units)), dma((layers, n_units)), dma((layers, n_units)), dma((layers, n_units)),
                   dma((layers, n_out // 2, 2)), dma((layers, n_out // 2, 2)),
                   dma((layers, n_out // 2, 2)), dma((layers, n_out // 2, 2)),
                   dma((layers, n_hb)), dma((layers, n_hb)), dma((layers, n_hb)), dma((layers, n_hb)),
                   dma((layers,)), dma((layers,)), dma((layers,)), dma((layers,)),
                   dma((layers, n_out, 2)), dma((layers, n_out, 2)), dma((layers, n_out)), dma((layers, n_out)),
                   dma((2,)), dma((2,)), dma((2,)), dma((2, 4)), dma((2,)), dma((2,)), dma((4,)), dma((2, 4)), dma((4,)),
                   dma((2, 6)), dma((4,)), dma((3,))]
        hbm = pl.BlockSpec(memory_space=pl.ANY)
        kernel = make_kernel(rows, seqs, d, dh, block_in, aw, ff, n_units)
        got = pl.pallas_call(
            kernel, out_shape=outs, in_specs=[hbm] * 6, out_specs=[hbm] * len(outs), scratch_shapes=scratch, name='two_layers',
            compiler_params=pltpu.CompilerParams(collective_id=0, has_side_effects=True, vmem_limit_bytes=67_000_000),
        )(x_loc.reshape(rows, d), lens, gain, w_in_loc, w_attn_loc, w_mlp_loc)
        return got[0].reshape(seqs, pos, d)

    return jax.shard_map(device_step, mesh=mesh,
                         in_specs=(P(batch_axes, 'model', None), P(batch_axes), P(None, 'data'), P(None, 'data', 'model'),
                                   P(None, 'model', 'data'), P(None, 'model', 'data')),
                         out_specs=P(batch_axes, 'model', None), check_vma=False)
```

time: 3660 us -> 2110 us (0.58)
  waiting for transfers between devices: 2330 us -> 0 us
  Pallas kernels: 0 us -> 2100 us
  matrix products: 1120 us -> 0 us
  other arithmetic: 99.3 us -> 0 us
  local copies, waits for them, and re-layouts: 77.8 us -> 10.6 us
    pallas_call x0 -> x1, Pallas kernels: none -> 2100 us  [device_step(): pl.pallas_call(kernel, out_shape=outs, in_specs=[hbm] * 6, out_specs=[hbm...]
    all_gather x8 -> x0, waiting for transfers between devices: 1880 us -> none  [the longest x2 1550 us: device_step(): w_in_full = lax.all_gather(w_in_loc[layer_idx], 'data', axis=0, tiled=True)]
    dot_general x10 -> x0, matrix products: 1120 us -> none  [the longest x2 629 us: device_step(): jnp.dot(h_full, w_in_full, preferred_element_type=jnp.float32)]
    reduce_scatter x2 -> x0, waiting for transfers between devices: 447 us -> none  [device_step(): lax.psum_scatter(group_part, 'model', scatter_dimension=1, tiled=True)]
    slice x4 -> x0, local copies, waits for them, and re-layouts: 74.3 us -> none  [the longest x1 44.6 us: device_step(): w_in_full = lax.all_gather(w_in_loc[layer_idx], 'data', axis=0, tiled=True)]
    reduce_sum x6 -> x0, other arithmetic: 64.1 us -> none  [the longest x2 44 us: device_step(): soft_probs = jax.nn.softmax(scores, axis=-1)]
  transfers between devices with their start and end apart: 10 -> 0, of which waited for: 6 -> 0; matrix products, arithmetic and copies ran while one was open for 32% -> 0% of each run, Pallas kernels for 0% -> 0%
where the time goes in v1:
time: 2110 us
  Pallas kernels  2100 us (100%)
    pallas_call x1, Pallas kernels, device_step(): pl.pallas_call(kernel, out_shape=outs, in_specs=[hbm] * 6, out_specs=[hbm...  2100 us

profile of v1, /device:TPU:0, one launch (start us, length us, event | category | flops | bytes accessed | tf_op | source)
XLA Modules:
  0.0 2112.2 jit_solution(12808660918286106331)
XLA Ops:
  0.0 1.3 broadcast_in_dim.4.lens
  1.3 1.4 broadcast_in_dim.5.gain
  2.7 2101.6 %two_layers.1 = (bf16[1024,4096]{1,0:T(8,128)(2,1)}, bf16[2,2048,8448]{2,1,0:T(8,128)(2,1)}, bf16[2,1024,2048]{2,1,0:T(8,128)(2,1)}, bf16[2,3584,2048]{2,1,0:T(8...) custom-call(bf16[1024,4096]{1,0:T(8,128)(2,1)} %bitcast.2, ...), custom_call_target="tpu_custom_call" | custom-call | tf_op jit(solution)/shard_map/two_layers/pallas_call | solution.py:643
  2104.3 7.9 copy.8

commit v2 on v1

--- a/solution.py
+++ b/solution.py
@@ -9,6 +9,7 @@
 HEAD = 128
 UNIT = 256
 TILE = 512
+SOFT = 32
 NEG = -1e30
 MESH = pl.DeviceIdType.MESH
 BF = jnp.bfloat16
@@ -26,8 +27,7 @@
     n_out = d // TILE
     n_half = n_out // 2
     pos = rows // seqs
-    early = 8
-    visits = 2 * early + (n_gu - early)
+    early0, early1 = 8, 11
     kk = aw + ff
     lnr = 64
     n_ln = rows // lnr
@@ -36,10 +36,10 @@
     qscale = HEAD ** -0.5 * 1.4426950408889634
 
     def kernel(x, lens, gain, w_in, w_at, w_ml,
-               y_out, a_in, a_at, a_ml, r_in, r_at, r_ml, h_all, kvb, q_b, m_b, z_b, xr, yq, yr, hid,
-               big, wv, ov, xin, hst, gv, lv, qv, kvv,
+               y_out, a_in, a_at, a_ml, r_in, r_at, r_ml, h_all, kvb, q_b, m_b, z_b, xr, sq, ym, yr, hid,
+               big, wv, ov, ab, xin, hst, gv, lv, qv, kvv, sv,
                a_s, a_r, wy_s, wy_r, wc_s, wc_r, oy_s, oy_r, oc_s, oc_r, hy_s, hy_r, hx_s, hx_r, hf_s, hf_r,
-               kv_s, kv_r, xz_s, xz_r, yz_s, yz_r, g_s, g_r, lg, li, lh, lo, hl, ws, os_, ai, ml_s, ad):
+               kv_s, kv_r, xz_s, xz_r, yz_s, yz_r, y3_s, y3_r, g_s, g_r, lg, li, lh, lo, hl, ws, os_, ai, ml_s, ad):
         rep = lax.axis_index('rep')
         y = lax.axis_index('data')
         m = lax.axis_index('model')
@@ -108,7 +108,19 @@
             return remote(z_b.at[l, 2 + i, :, tcols(t)], xr.at[l, i, :, tcols(t)], xz_s.at[l, t, i], xz_r.at[l, t, i], xpeer)
 
         def yz(l, t):
-            return remote(yq.at[l, :, tcols(t)], yr.at[l, :, tcols(t)], yz_s.at[l, t], yz_r.at[l, t], ypeer)
+            return remote(sq.at[l, :, tcols(t)], yr.at[l, :, tcols(t)], yz_s.at[l, t], yz_r.at[l, t], ypeer)
+
+        def yz_first(l, t):
+            return remote(z_b.at[l, 1, :, tcols(t)], yr.at[l, :, tcols(t)], yz_s.at[l, t], yz_r.at[l, t], ypeer)
+
+        def yz_pass(l, t):
+            return remote(z_b.at[l, 3, :, tcols(t)], ym.at[:, tcols(t)], y3_s.at[t], y3_r.at[t], ypeer)
+
+        def xz_last(l, t):
+            return remote(sq.at[l, :, tcols(t)], xr.at[l, 0, :, tcols(t)], xz_s.at[l, t, 0], xz_r.at[l, t, 0], xpeer)
+
+        def y_goes_first(l, t):
+            return jnp.logical_and(l == 1, lax.rem(t, n_half) == n_half - 1)
 
         def issue_gu(l, j):
             wy(l, gate_u + j).start()
@@ -188,10 +200,8 @@
             return pl.ds(pl.multiple_of(r * lnr, lnr), lnr)
 
         def ln_phase(kind):
-            l = 0 if kind == 0 else kind - 1
-            ln = 1 if kind == 1 else 0
-            base = hid if kind == 2 else x
-            srcs = [base] if kind == 0 else [base, z_b.at[l, 0], xr.at[l, 0], yr.at[l]]
+            ln = kind
+            srcs = [x, z_b.at[0, 0], xr.at[0, 0], yr.at[0]] if kind else [x]
 
             def loads(r, slot):
                 return [local(s.at[lrows(r)], xin.at[slot, i], li.at[slot, i]) for i, s in enumerate(srcs)]
@@ -200,7 +210,7 @@
                 return local(big.at[0, lrows(r), 0:d], h_all.at[ln, 0, lrows(r)], lh.at[slot])
 
             def store_o(r, slot):
-                return local(hst.at[slot], (hid if kind == 1 else y_out).at[lrows(r)], lo.at[slot])
+                return local(hst.at[slot], hid.at[lrows(r)], lo.at[slot])
 
             def send(b):
                 hy(ln, b).start()
@@ -231,7 +241,7 @@
                         v = (v + (zs + xin[slot, 3, rs, :].astype(F32))).astype(BF)
                         hst[slot, rs, :] = v
                         v = v.astype(F32)
-                    if kind < 2:
+                    if True:
                         mean = jnp.sum(v, axis=-1, keepdims=True) * (1.0 / d)
                         cen = v - mean
                         var = jnp.sum(cen * cen, axis=-1, keepdims=True) * (1.0 / d)
@@ -240,7 +250,7 @@
                 loop(0, lnr // 32, sub)
                 if kind > 0:
                     store_o(r, slot).start()
-                if kind < 2:
+                if True:
                     store_h(r, slot).start()
 
                     @pl.when(r >= 1)
@@ -254,9 +264,8 @@
             if kind > 0:
                 store_o(n_ln - 2, 0).wait()
                 store_o(n_ln - 1, 1).wait()
-            if kind < 2:
-                store_h(n_ln - 1, 1).wait()
-                send(n_hb - 1)
+            store_h(n_ln - 1, 1).wait()
+            send(n_hb - 1)
 
         barrier = pltpu.get_barrier_semaphore()
         for dev in (ypeer, xpeer, cpeer):
@@ -326,6 +335,9 @@
             def m_store(s, j):
                 return local(ov.at[s, :, 0:UNIT], m_b.at[s, :, ucols(j)], os_.at[s])
 
+            early = early0 + (early1 - early0) * l
+            visits = n_gu + early
+
             def visit(v):
                 slot = lax.rem(v, 2)
                 wait_unit(slot, 0)
@@ -361,7 +373,7 @@
                         @pl.when(nv == visits)
                         def _():
                             arrive(l, kv_u)
-                            load_unit(l, kv_u, visits % 2, 0)
+                            load_unit(l, kv_u, lax.rem(visits, 2), 0)
 
                     @pl.when(v != early * lax.div(s, 3))
                     def _():
@@ -374,7 +386,7 @@
                 loop(s_lo, s_hi, shard)
             loop(0, visits, visit)
 
-            kslot = visits % 2
+            kslot = lax.rem(n_gu + early, 2)
             wait_unit(kslot, 0)
 
             def kv_store(s):
@@ -396,7 +408,7 @@
                 return local(ov.at[s], q_b.at[s, :, tcols(t)], os_.at[s])
 
             def q_tile(t):
-                slot = lax.rem(t + 1 - kslot, 2)
+                slot = lax.rem(t + 1 + kslot, 2)
                 wait_unit(slot, 0)
                 wait_unit(slot, 1)
 
@@ -428,7 +440,7 @@
             def m_load(s):
                 return local(m_b.at[s], big.at[s, :, aw:kk], ml_s.at[s])
             loop(0, 4, lambda s: m_load(s).start())
-            oslot = (1 - kslot + n_q) % 2
+            oslot = lax.rem(1 + kslot + n_q, 2)
             load_o_near(l, 0, oslot)
             kvx(l).wait_recv()
 
@@ -463,21 +475,30 @@
                 row = pl.ds(pl.multiple_of(b * pos, pos), pos)
                 for blk in range(2):
                     nk = 2 * pos * (blk + 1)
-                    qpos = lax.broadcasted_iota(jnp.int32, (pos, nk), 0) + (2 * blk + c) * pos
-                    kpos = lax.broadcasted_iota(jnp.int32, (pos, nk), 1)
-                    ok = jnp.logical_and(kpos <= qpos, kpos < lv[a, pl.ds(b, 1), 0:nk])
                     keys = kvv[slot, 0:nk, 0:HEAD]
                     vals = kvv[slot, 0:nk, HEAD:2 * HEAD]
                     sh = a + 2 * (blk + xx - 2 * blk * xx)
+                    q_all = jnp.concatenate([qv[slot, blk, :, hd * HEAD:(hd + 1) * HEAD] for hd in range(q_heads)], axis=0)
+                    sv[:, 0:nk] = lax.dot_general(q_all, keys, (((1,), (1,)), ((), ())), preferred_element_type=F32)
+
+                    def head(hd):
+                        for part in range(pos // SOFT):
+                            r0 = part * SOFT
+                            rs = slice(hd * pos + r0, hd * pos + r0 + SOFT)
+                            qpos = lax.broadcasted_iota(jnp.int32, (SOFT, 2 * pos), 0) + ((2 * blk + c) * pos + r0)
+                            kpos = lax.broadcasted_iota(jnp.int32, (SOFT, 2 * pos), 1) + (nk - 2 * pos)
+                            last = jnp.minimum(qpos, lv[a, pl.ds(b, 1), 0:2 * pos] - 1)
+                            s = sv[rs, nk - 2 * pos:nk] * qscale
+                            s = jnp.where(kpos <= last, s, NEG)
+                            if blk:
+                                s = jnp.concatenate([sv[rs, 0:2 * pos] * qscale, s], axis=1)
+                            e = jnp.exp2(s - jnp.max(s, axis=-1, keepdims=True))
+                            ov[0, rs, 0:nk] = (e / jnp.sum(e, axis=-1, keepdims=True)).astype(BF)
                     for hd in range(q_heads):
-                        cs = slice(hd * HEAD, (hd + 1) * HEAD)
-                        s = lax.dot_general(qv[slot, blk, :, cs], keys, (((1,), (1,)), ((), ())),
-                                            preferred_element_type=F32) * qscale
-                        s = jnp.where(ok, s, NEG)
-                        e = jnp.exp2(s - jnp.max(s, axis=-1, keepdims=True))
-                        den = jnp.sum(e, axis=-1, keepdims=True)
-                        o = jnp.dot(e.astype(BF), vals, preferred_element_type=F32)
-                        big[sh, row, cs] = (o / den).astype(BF)
+                        head(hd)
+                    o = jnp.dot(ov[0, :, 0:nk], vals, preferred_element_type=F32).astype(BF)
+                    for hd in range(q_heads):
+                        big[sh, row, hd * HEAD:(hd + 1) * HEAD] = o[hd * pos:(hd + 1) * pos]
             loop(0, 2 * seqs, seq)
 
             @pl.when(jnp.logical_and(giver, l == 0))
@@ -489,15 +510,56 @@
                 return lax.rem(y + lax.div(k, n_half), 2) * n_half + lax.rem(k, n_half)
 
             def z_store(s, t):
-                return local(ov.at[s], z_b.at[l, s, :, tcols(t)], os_.at[s])
+                return local(ov.at[s], z_b.at[l, s, :, tcols(t)], os_.at[0])
+
+            def add_tile(k):
+                t = tau(k)
+                first = y_goes_first(l, t)
+
+                def total(lhs_ref, rhs_ref):
+                    lhs = local(lhs_ref, ab.at[0], ad.at[0])
+                    rhs = local(rhs_ref, ab.at[1], ad.at[1])
+                    lhs.start()
+                    rhs.start()
+                    lhs.wait()
+                    rhs.wait()
+
+                    def sub(i):
+                        rs = pl.ds(pl.multiple_of(i * 128, 128), 128)
+                        ab[0, rs, :] = (ab[0, rs, :].astype(F32) + ab[1, rs, :].astype(F32)).astype(BF)
+                    loop(0, rows // 128, sub)
+                    out = local(ab.at[0], sq.at[l, :, tcols(t)], ad.at[2])
+                    out.start()
+                    out.wait()
+
+                @pl.when(jnp.logical_not(first))
+                def _():
+                    xz(l, t, 0).wait_recv()
+                    xz(l, t, 1).wait_recv()
+                    total(z_b.at[l, 1, :, tcols(t)], xr.at[l, 1, :, tcols(t)])
+                    yz(l, t).start()
+
+                @pl.when(first)
+                def _():
+                    yz_pass(l, t).wait_recv()
+                    total(z_b.at[l, 2, :, tcols(t)], ym.at[:, tcols(t)])
+                    xz_last(l, t).start()
+
+                @pl.when(jnp.logical_and(giver, jnp.logical_and(l == 0, jnp.logical_and(lax.rem(k, 2) == 1, k >= 3))))
+                def _():
+                    issue_gu(1, 2 + lax.div(k - 3, 2))
 
             def out_tile(k):
                 slot = lax.rem(k + oslot, 2)
                 t = tau(k)
+                first = y_goes_first(l, t)
                 wait_o(slot)
 
+                def order(si):
+                    return si + 2 - lax.div(si, 2) * (2 * si - 1)
+
                 def shard(si):
-                    s = lax.rem(si + 2, 4)
+                    s = order(si)
 
                     @pl.when(jnp.logical_and(si == 2, k + 1 < n_half))
                     def _():
@@ -508,49 +570,42 @@
                         arrive_o(l, k + 1 - n_half)
                         load_o(l, r_at, r_ml, k + 1 - n_half, 1 - slot)
 
-                    @pl.when(jnp.logical_and(si >= 2, k > 0))
-                    def _():
-                        z_store(s, t).wait()
-
-                    @pl.when(jnp.logical_and(si >= 1, si < 3))
-                    def _():
-                        z_store(si + 1, t).wait()
-                        xz(l, t, si - 1).start()
                     acc = jnp.dot(big[s], wv[slot], preferred_element_type=F32)
                     ov[s] = acc.astype(BF)
+
+                    @pl.when(jnp.logical_or(si > 0, k > 0))
+                    def _():
+                        z_store(0, t).wait()
+
+                    @pl.when(jnp.logical_and(jnp.logical_not(first), jnp.logical_and(si >= 1, si < 3)))
+                    def _():
+                        xz(l, t, si - 1).start()
+
+                    @pl.when(jnp.logical_and(first, si == 2))
+                    def _():
+                        yz_pass(l, t).start()
+
+                    @pl.when(jnp.logical_and(first, si == 3))
+                    def _():
+                        yz_first(l, t).start()
                     z_store(s, t).start()
                 loop(0, 4, shard)
+
+                @pl.when(jnp.logical_and(k >= 3, lax.rem(k, 2) == 1))
+                def _():
+                    add_tile(lax.div(k - 3, 2))
             loop(0, n_out, out_tile)
-            loop(0, 2, lambda s: z_store(s, 0).wait())
-
-            def add_tile(k):
-                t = tau(k)
-                xz(l, t, 0).wait_recv()
-                xz(l, t, 1).wait_recv()
-                lhs = local(z_b.at[l, 1, :, tcols(t)], ov.at[0], ad.at[0])
-                rhs = local(xr.at[l, 1, :, tcols(t)], ov.at[1], ad.at[1])
-                lhs.start()
-                rhs.start()
-                lhs.wait()
-                rhs.wait()
-
-                def sub(i):
-                    rs = pl.ds(pl.multiple_of(i * 128, 128), 128)
-                    ov[0, rs, :] = (ov[0, rs, :].astype(F32) + ov[1, rs, :].astype(F32)).astype(BF)
-                loop(0, rows // 128, sub)
-                out = local(ov.at[0], yq.at[l, :, tcols(t)], ad.at[2])
-                out.start()
-                out.wait()
-                yz(l, t).start()
-
-                @pl.when(jnp.logical_and(giver, jnp.logical_and(l == 0, k >= 5)))
-                def _():
-                    issue_gu(1, k - 3)
-            loop(0, n_out, add_tile)
-            loop(0, n_out, lambda t: yz(l, t).wait_recv())
+            z_store(0, 0).wait()
+
+            loop(3, n_out, add_tile)
+
+            @pl.when(jnp.logical_and(giver, l == 0))
+            def _():
+                pass
 
             @pl.when(l == 0)
             def _():
+                loop(0, n_out, lambda t: yz(l, t).wait_recv())
                 ln_phase(1)
 
                 @pl.when(giver)
@@ -561,7 +616,29 @@
 
             @pl.when(l == 1)
             def _():
-                ln_phase(2)
+                def last_tile(k):
+                    t = lax.rem(1 - y + lax.div(k, n_half), 2) * n_half + lax.rem(k, n_half)
+
+                    @pl.when(y_goes_first(l, t))
+                    def _():
+                        xz(l, t, 0).wait_recv()
+                    yz(l, t).wait_recv()
+                    parts = (hid.at[:, tcols(t)], z_b.at[l, 0, :, tcols(t)], xr.at[l, 0, :, tcols(t)], yr.at[l, :, tcols(t)])
+                    cps = [local(p, ov.at[i], os_.at[i]) for i, p in enumerate(parts)]
+                    for cp in cps:
+                        cp.start()
+                    for cp in cps:
+                        cp.wait()
+
+                    def sub(i):
+                        rs = pl.ds(pl.multiple_of(i * 64, 64), 64)
+                        zs = ov[1, rs, :].astype(F32) + ov[2, rs, :].astype(F32)
+                        ov[0, rs, :] = (ov[0, rs, :].astype(F32) + (zs + ov[3, rs, :].astype(F32))).astype(BF)
+                    loop(0, rows // 64, sub)
+                    out = local(ov.at[0], y_out.at[:, tcols(t)], lo.at[0])
+                    out.start()
+                    out.wait()
+                loop(0, n_out, last_tile)
 
             def sent_h(b):
                 hy(l, b).wait_send()
@@ -572,8 +649,15 @@
 
             def sent_z(t):
                 xz(l, t, 0).wait_send()
-                xz(l, t, 1).wait_send()
                 yz(l, t).wait_send()
+
+                @pl.when(y_goes_first(l, t))
+                def _():
+                    yz_pass(l, t).wait_send()
+
+                @pl.when(jnp.logical_not(y_goes_first(l, t)))
+                def _():
+                    xz(l, t, 1).wait_send()
             loop(0, n_out, sent_z)
 
             @pl.when(giver)
@@ -622,13 +706,14 @@
         outs = [buf(rows, d), buf(layers, dh, block_in), buf(layers, aw, dh), buf(layers, ff, dh),
                 buf(layers, dh, block_in), buf(layers, aw, dh), buf(layers, ff, dh),
                 buf(layers, 4, rows, d), buf(layers, 2, 4, rows, 2 * HEAD), buf(4, rows, aw), buf(4, rows, ff),
-                buf(layers, 4, rows, d), buf(layers, 2, rows, d), buf(layers, rows, d), buf(layers, rows, d), buf(rows, d)]
+                buf(layers, 4, rows, d), buf(layers, 2, rows, d), buf(layers, rows, d), buf(rows, d), buf(layers, rows, d), buf(rows, d)]
         dma = pltpu.SemaphoreType.DMA
         n_hb = rows // 128
         scratch = [pltpu.VMEM((4, rows, kk), BF), pltpu.VMEM((2, kk, TILE), BF), pltpu.VMEM((4, rows, TILE), BF),
+                   pltpu.VMEM((2, rows, TILE), BF),
                    pltpu.VMEM((2, 4, 64, d), BF), pltpu.VMEM((2, 64, d), BF), pltpu.VMEM((layers, 8, d), F32),
                    pltpu.VMEM((2, seqs, seq_len), jnp.int32), pltpu.VMEM((2, 2, pos, aw), BF),
-                   pltpu.VMEM((2, seq_len, 2 * HEAD), BF),
+                   pltpu.VMEM((2, seq_len, 2 * HEAD), BF), pltpu.VMEM((rows, seq_len), F32),
                    dma((layers, 3)), dma((layers, 3)),
                    dma((layers, n_units)), dma((layers, n_units)), dma((layers, n_units)), dma((layers, n_units)),
                    dma((layers, n_out // 2, 2)), dma((layers, n_out // 2, 2)),
@@ -636,6 +721,7 @@
                    dma((layers, n_hb)), dma((layers, n_hb)), dma((layers, n_hb)), dma((layers, n_hb)),
                    dma((layers,)), dma((layers,)), dma((layers,)), dma((layers,)),
                    dma((layers, n_out, 2)), dma((layers, n_out, 2)), dma((layers, n_out)), dma((layers, n_out)),
+                   dma((n_out,)), dma((n_out,)),
                    dma((2,)), dma((2,)), dma((2,)), dma((2, 4)), dma((2,)), dma((2,)), dma((4,)), dma((2, 4)), dma((4,)),
                    dma((2, 6)), dma((4,)), dma((3,))]
         hbm = pl.BlockSpec(memory_space=pl.ANY)

time: 2110 us -> 1970 us (0.934)
  Pallas kernels: 2100 us -> 1950 us
    pallas_call x1, Pallas kernels: 2100 us -> 1950 us  [device_step(): pl.pallas_call(kernel, out_shape=outs, in_specs=[hbm] * 6, out_specs=[hbm...]
where the time goes in v2:
time: 1970 us; the launch traced here: 1960 us
  Pallas kernels  1950 us (99%)
    pallas_call x1, Pallas kernels, device_step(): pl.pallas_call(kernel, out_shape=outs, in_specs=[hbm] * 6, out_specs=[hbm...  1950 us

profile of v2, /device:TPU:0, one launch (start us, length us, event | category | flops | bytes accessed | tf_op | source)
XLA Modules:
  0.0 1964.9 jit_solution(760350630976989967)
XLA Ops:
  0.0 1.3 broadcast_in_dim.4.lens
  1.3 1.4 broadcast_in_dim.5.gain
  2.7 1954.4 %two_layers.1 = (bf16[1024,4096]{1,0:T(8,128)(2,1)}, bf16[2,2048,8448]{2,1,0:T(8,128)(2,1)}, bf16[2,1024,2048]{2,1,0:T(8,128)(2,1)}, bf16[2,3584,2048]{2,1,0:T(8...) custom-call(bf16[1024,4096]{1,0:T(8,128)(2,1)} %bitcast.2, ...), custom_call_target="tpu_custom_call" | custom-call | tf_op jit(solution)/shard_map/two_layers/pallas_call | solution.py:729
  1957.1 7.9 copy.8

commit v3 on v2

--- a/solution.py
+++ b/solution.py
@@ -27,19 +27,20 @@
     n_out = d // TILE
     n_half = n_out // 2
     pos = rows // seqs
-    early0, early1 = 8, 11
     kk = aw + ff
     lnr = 64
+    early0, early1 = 6, 10
+    n_own = 2
     n_ln = rows // lnr
     n_hb = n_ln // 2
     hb = 2 * lnr
     qscale = HEAD ** -0.5 * 1.4426950408889634
 
     def kernel(x, lens, gain, w_in, w_at, w_ml,
-               y_out, a_in, a_at, a_ml, r_in, r_at, r_ml, h_all, kvb, q_b, m_b, z_b, xr, sq, ym, yr, hid,
+               y_out, a_in, a_at, a_ml, r_in, r_at, r_ml, h_all, kvb, q_b, m_b, z_b, xr, sq, ym, yr, hid, o_b,
                big, wv, ov, ab, xin, hst, gv, lv, qv, kvv, sv,
                a_s, a_r, wy_s, wy_r, wc_s, wc_r, oy_s, oy_r, oc_s, oc_r, hy_s, hy_r, hx_s, hx_r, hf_s, hf_r,
-               kv_s, kv_r, xz_s, xz_r, yz_s, yz_r, y3_s, y3_r, g_s, g_r, lg, li, lh, lo, hl, ws, os_, ai, ml_s, ad):
+               kv_s, kv_r, xz_s, xz_r, yz_s, yz_r, y3_s, y3_r, g_s, g_r, lg, li, lh, lo, hl, ws, os_, ai, ao, ml_s, ol_s, ad):
         rep = lax.axis_index('rep')
         y = lax.axis_index('data')
         m = lax.axis_index('model')
@@ -101,8 +102,8 @@
         def hf(l):
             return remote(h_all.at[l, 1], h_all.at[l, 3], hf_s.at[l], hf_r.at[l], xpeer)
 
-        def kvx(l):
-            return remote(kvb.at[l, 0], kvb.at[l, 1], kv_s.at[l], kv_r.at[l], cpeer)
+        def kvx(l, a):
+            return remote(kvb.at[l, 0, a], kvb.at[l, 1, a], kv_s.at[l, a], kv_r.at[l, a], cpeer)
 
         def xz(l, t, i):
             return remote(z_b.at[l, 2 + i, :, tcols(t)], xr.at[l, i, :, tcols(t)], xz_s.at[l, t, i], xz_r.at[l, t, i], xpeer)
@@ -126,9 +127,11 @@
             wy(l, gate_u + j).start()
             wy(l, up_u + j).start()
 
-        def issue_qkv(l):
+        def issue_kv(l):
             wy(l, kv_u).start()
-            loop(0, kv_u, lambda u: wy(l, u).start())
+
+        def issue_q(l, u_lo):
+            loop(u_lo, kv_u, lambda u: wy(l, u).start())
 
         def issue_o(l, t):
             for cp in oy(l, t):
@@ -298,7 +301,8 @@
 
         @pl.when(giver)
         def _():
-            issue_gu(0, 0)
+            issue_kv(0)
+            wy(0, 0).start()
         gain_l().wait()
         lens_l().wait()
         gain_y().wait()
@@ -307,8 +311,8 @@
 
         @pl.when(giver)
         def _():
-            loop(1, n_gu, lambda j: issue_gu(0, j))
-            issue_qkv(0)
+            issue_q(0, 1)
+            loop(0, n_gu, lambda j: issue_gu(0, j))
             loop(0, n_half, lambda t: issue_o(0, t))
 
         def layer(l):
@@ -319,173 +323,206 @@
 
             def h_load(s):
                 return local(h_all.at[l, s], big.at[s, :, 0:d], hl.at[s])
+
+            def m_store(s, j, buf):
+                return local(ov.at[buf, :, 0:UNIT], m_b.at[s, :, ucols(j)], os_.at[0])
+
+            def q_store(s, t, buf):
+                return local(ov.at[buf], q_b.at[s, :, tcols(t)], os_.at[0])
+
+            def kv_store(s, buf):
+                return local(ov.at[buf, :, 0:UNIT], kvb.at[l, 0, lax.rem(s, 2), lax.div(s, 2)], os_.at[0])
+
+            def wait_half():
+                m_store(0, 0, 0).wait()
+
+            def wait_full():
+                q_store(0, 0, 0).wait()
+
+            def arrive_gu(j):
+                arrive(l, gate_u + j)
+                arrive(l, up_u + j)
+
+            def load_gu(j, slot):
+                load_unit(l, gate_u + j, slot, 0)
+                load_unit(l, up_u + j, slot, 1)
+
+            def arrive_q(t):
+                arrive(l, 2 * t)
+                arrive(l, 2 * t + 1)
+
+            def load_q(t, slot):
+                load_unit(l, 2 * t, slot, 0)
+                load_unit(l, 2 * t + 1, slot, 1)
+
+            def load_kv(slot):
+                load_unit(l, kv_u, slot, 0)
+
+            def wait_tile(slot):
+                wait_unit(slot, 0)
+                wait_unit(slot, 1)
+
+            def gu_step(s, j, slot, before, buf):
+                acc = jnp.dot(big[s, :, 0:d], wv[slot, 0:d, :], preferred_element_type=F32)
+                g = acc[:, :UNIT].astype(BF).astype(F32)
+                u = acc[:, UNIT:].astype(BF).astype(F32)
+                ov[buf, :, 0:UNIT] = (g * jax.nn.sigmoid(g) * u).astype(BF)
+                before()
+                m_store(s, j, buf).start()
+
+            def q_step(s, t, slot, before, buf):
+                ov[buf] = jnp.dot(big[s, :, 0:d], wv[slot, 0:d, :], preferred_element_type=F32).astype(BF)
+                before()
+                q_store(s, t, buf).start()
+
+            def kv_step(s, slot, before, buf):
+                ov[buf, :, 0:UNIT] = jnp.dot(big[s, :, 0:d], wv[slot, 0:d, 0:UNIT], preferred_element_type=F32).astype(BF)
+                before()
+                kv_store(s, buf).start()
+
+            def nothing():
+                pass
+
+            def either(cond, yes, no):
+                def go():
+                    pl.when(cond)(yes)
+                    pl.when(jnp.logical_not(cond))(no)
+                return go
+
+            def unless(cond, no):
+                return lambda: pl.when(jnp.logical_not(cond))(no)
+
+            @pl.when(l == 0)
+            def _():
+                arrive(l, kv_u)
+                load_kv(0)
+
+            @pl.when(l == 1)
+            def _():
+                arrive(l, kv_u)
+                load_kv(0)
+                arrive_q(0)
+                load_q(0, 1)
+                wait_unit(0, 0)
+                kv_step(0, 0, nothing, 0)
+
+                def own_q(t):
+                    slot = lax.rem(1 + t, 2)
+
+                    @pl.when(t + 1 < n_q)
+                    def _():
+                        arrive_q(t + 1)
+                        load_q(t + 1, 1 - slot)
+
+                    @pl.when(t + 1 == n_q)
+                    def _():
+                        arrive_gu(0)
+                        load_gu(0, 1 - slot)
+                    wait_tile(slot)
+                    q_step(0, t, slot, either(t == 0, wait_half, wait_full), slot)
+                loop(0, n_q, own_q)
+
+                def own_gu(j):
+                    slot = lax.rem(1 + j, 2)
+
+                    @pl.when(j + 1 < n_own)
+                    def _():
+                        arrive_gu(j + 1)
+                        load_gu(j + 1, 1 - slot)
+                    wait_tile(slot)
+                    gu_step(0, j, slot, either(j == 0, wait_full, wait_half), slot)
+                loop(0, n_own, own_gu)
+                wait_half()
+                load_kv(0)
 
             loop(0, n_hb, lambda b: hy(l, b).wait_recv())
             hf(l).start()
             h_load(1).start()
             loop(0, n_hb, lambda b: hx(l, b).wait_recv())
             h_load(2).start()
-            arrive(l, gate_u)
-            arrive(l, up_u)
-            load_unit(l, gate_u, 0, 0)
-            load_unit(l, up_u, 0, 1)
             h_load(1).wait()
             h_load(2).wait()
 
-            def m_store(s, j):
-                return local(ov.at[s, :, 0:UNIT], m_b.at[s, :, ucols(j)], os_.at[s])
-
-            early = early0 + (early1 - early0) * l
-            visits = n_gu + early
-
-            def visit(v):
-                slot = lax.rem(v, 2)
-                wait_unit(slot, 0)
-                wait_unit(slot, 1)
-                blk = lax.div(v, early)
-                j = v - early * lax.div(lax.min(blk, 2) + 1, 2)
-                s_lo = 3 * lax.rem(lax.min(blk, 2), 2)
-                s_hi = 3 + lax.div(lax.min(blk, 2) + 1, 2)
-                s_pf = s_lo + lax.div(s_hi - s_lo, 2)
-
-                @pl.when(v == early)
-                def _():
-                    hf(l).wait_recv()
-                    h_load(3).start()
-                    h_load(3).wait()
+            wait_unit(0, 0)
+
+            def kv_a(s):
+                @pl.when(s == 1)
+                def _():
+                    pl.when(l == 0)(lambda: arrive_q(0))
+                    load_q(0, 1)
+                kv_step(s, 0, unless(s == l, wait_half), s)
+            loop(l, 3, kv_a)
+
+            def q_a(t):
+                slot = lax.rem(1 + t, 2)
+                wait_tile(slot)
 
                 def shard(s):
-                    @pl.when(s == s_pf)
-                    def _():
-                        nv = v + 1
-                        nj = nv - early * lax.div(lax.min(lax.div(nv, early), 2) + 1, 2)
-
-                        @pl.when(jnp.logical_and(lax.div(nv, early) != 1, nv < visits))
-                        def _():
-                            arrive(l, gate_u + nj)
-                            arrive(l, up_u + nj)
-
-                        @pl.when(nv < visits)
-                        def _():
-                            load_unit(l, gate_u + nj, 1 - slot, 0)
-                            load_unit(l, up_u + nj, 1 - slot, 1)
-
-                        @pl.when(nv == visits)
-                        def _():
-                            arrive(l, kv_u)
-                            load_unit(l, kv_u, lax.rem(visits, 2), 0)
-
-                    @pl.when(v != early * lax.div(s, 3))
-                    def _():
-                        m_store(s, 0).wait()
-                    acc = jnp.dot(big[s, :, 0:d], wv[slot, 0:d, :], preferred_element_type=F32)
-                    g = acc[:, :UNIT].astype(BF).astype(F32)
-                    u = acc[:, UNIT:].astype(BF).astype(F32)
-                    ov[s, :, 0:UNIT] = (g * jax.nn.sigmoid(g) * u).astype(BF)
-                    m_store(s, j).start()
-                loop(s_lo, s_hi, shard)
-            loop(0, visits, visit)
-
-            kslot = lax.rem(n_gu + early, 2)
-            wait_unit(kslot, 0)
-
-            def kv_store(s):
-                return local(ov.at[s, :, 0:UNIT], kvb.at[l, 0, s], os_.at[s])
-
-            def kv_shard(s):
-                @pl.when(s == 2)
-                def _():
-                    for u in range(2):
-                        arrive(l, u)
-                        load_unit(l, u, 1 - kslot, u)
-                m_store(s, 0).wait()
-                acc = jnp.dot(big[s, :, 0:d], wv[kslot, 0:d, 0:UNIT], preferred_element_type=F32)
-                ov[s, :, 0:UNIT] = acc.astype(BF)
-                kv_store(s).start()
-            loop(0, 4, kv_shard)
-
-            def q_store(s, t):
-                return local(ov.at[s], q_b.at[s, :, tcols(t)], os_.at[s])
-
-            def q_tile(t):
-                slot = lax.rem(t + 1 + kslot, 2)
-                wait_unit(slot, 0)
-                wait_unit(slot, 1)
-
-                def shard(s):
-                    @pl.when(jnp.logical_and(s == 2, t + 1 < n_q))
-                    def _():
-                        for i in range(2):
-                            arrive(l, 2 * (t + 1) + i)
-                            load_unit(l, 2 * (t + 1) + i, 1 - slot, i)
-
-                    @pl.when(t == 0)
-                    def _():
-                        kv_store(s).wait()
-
-                    @pl.when(t > 0)
-                    def _():
-                        q_store(s, 0).wait()
-                    acc = jnp.dot(big[s, :, 0:d], wv[slot, 0:d, :], preferred_element_type=F32)
-                    ov[s] = acc.astype(BF)
-                    q_store(s, t).start()
-                loop(0, 4, shard)
+                    @pl.when(jnp.logical_and(s == 1, t + 1 < n_q))
+                    def _():
+                        pl.when(l == 0)(lambda: arrive_q(t + 1))
+                        load_q(t + 1, 1 - slot)
+                    q_step(s, t, slot, either(jnp.logical_and(t == 0, s == l), wait_half, wait_full), s)
+                loop(l, 3, shard)
 
                 @pl.when(t == 0)
                 def _():
-                    kvx(l).start()
-            loop(0, n_q, q_tile)
-            loop(0, 4, lambda s: q_store(s, 0).wait())
-
-            def m_load(s):
-                return local(m_b.at[s], big.at[s, :, aw:kk], ml_s.at[s])
-            loop(0, 4, lambda s: m_load(s).start())
-            oslot = lax.rem(1 + kslot + n_q, 2)
-            load_o_near(l, 0, oslot)
-            kvx(l).wait_recv()
-
-            def at_loads(i, slot):
-                a = lax.div(i, seqs)
-                b = lax.rem(i, seqs)
-                rs = pl.ds(pl.multiple_of(b * pos, pos), pos)
-
-                def at(quarter):
-                    return kvv.at[slot, pl.ds(pl.multiple_of(quarter * pos, pos), pos)]
-                return (local(q_b.at[a, rs], qv.at[slot, xx], ai.at[slot, 0]),
-                        local(q_b.at[2 + a, rs], qv.at[slot, 1 - xx], ai.at[slot, 1]),
-                        local(kvb.at[l, 0, a, rs], at(2 * xx + c), ai.at[slot, 2]),
-                        local(kvb.at[l, 0, 2 + a, rs], at(2 * (1 - xx) + c), ai.at[slot, 3]),
-                        local(kvb.at[l, 1, a, rs], at(2 * xx + 1 - c), ai.at[slot, 4]),
-                        local(kvb.at[l, 1, 2 + a, rs], at(2 * (1 - xx) + 1 - c), ai.at[slot, 5]))
-
-            for cp in at_loads(0, 0):
-                cp.start()
-
-            def seq(i):
-                slot = lax.rem(i, 2)
-                a = lax.div(i, seqs)
-                b = lax.rem(i, seqs)
-
-                @pl.when(i + 1 < 2 * seqs)
-                def _():
-                    for cp in at_loads(i + 1, 1 - slot):
-                        cp.start()
-                for cp in at_loads(i, slot):
-                    cp.wait()
-                row = pl.ds(pl.multiple_of(b * pos, pos), pos)
-                for blk in range(2):
-                    nk = 2 * pos * (blk + 1)
-                    keys = kvv[slot, 0:nk, 0:HEAD]
-                    vals = kvv[slot, 0:nk, HEAD:2 * HEAD]
-                    sh = a + 2 * (blk + xx - 2 * blk * xx)
-                    q_all = jnp.concatenate([qv[slot, blk, :, hd * HEAD:(hd + 1) * HEAD] for hd in range(q_heads)], axis=0)
-                    sv[:, 0:nk] = lax.dot_general(q_all, keys, (((1,), (1,)), ((), ())), preferred_element_type=F32)
-
-                    def head(hd):
-                        for part in range(pos // SOFT):
-                            r0 = part * SOFT
-                            rs = slice(hd * pos + r0, hd * pos + r0 + SOFT)
-                            qpos = lax.broadcasted_iota(jnp.int32, (SOFT, 2 * pos), 0) + ((2 * blk + c) * pos + r0)
+                    kvx(l, 0).start()
+            loop(0, n_q, q_a)
+            wait_full()
+
+            def attend(a, middle):
+                kvx(l, a).wait_recv()
+
+                def at_loads(b, slot):
+                    rs = pl.ds(pl.multiple_of(b * pos, pos), pos)
+
+                    def at(quarter):
+                        return kvv.at[slot, pl.ds(pl.multiple_of(quarter * pos, pos), pos)]
+                    return (local(q_b.at[a, rs], qv.at[slot, xx], ai.at[slot, 0]),
+                            local(q_b.at[2 + a, rs], qv.at[slot, 1 - xx], ai.at[slot, 1]),
+                            local(kvb.at[l, 0, a, 0, rs], at(2 * xx + c), ai.at[slot, 2]),
+                            local(kvb.at[l, 0, a, 1, rs], at(2 * (1 - xx) + c), ai.at[slot, 3]),
+                            local(kvb.at[l, 1, a, 0, rs], at(2 * xx + 1 - c), ai.at[slot, 4]),
+                            local(kvb.at[l, 1, a, 1, rs], at(2 * (1 - xx) + 1 - c), ai.at[slot, 5]))
+
+                def o_stores(b, slot):
+                    rs = pl.ds(pl.multiple_of(b * pos, pos), pos)
+                    out = []
+                    for blk in range(2):
+                        sh = a + 2 * (blk + xx - 2 * blk * xx)
+                        for i in range(n_q):
+                            n = blk * n_q + i
+                            out.append(local(ab.at[slot, n * pos:(n + 1) * pos], o_b.at[sh, rs, i * TILE:(i + 1) * TILE], ao.at[slot, n]))
+                    return out
+
+                for cp in at_loads(0, 0):
+                    cp.start()
+
+                def seq(b):
+                    slot = lax.rem(b, 2)
+
+                    @pl.when(b + 1 < seqs)
+                    def _():
+                        for cp in at_loads(b + 1, 1 - slot):
+                            cp.start()
+                    pl.when(b == seqs // 2)(middle)
+                    for cp in at_loads(b, slot):
+                        cp.wait()
+
+                    @pl.when(b >= 2)
+                    def _():
+                        for cp in o_stores(b - 2, slot):
+                            cp.wait()
+                    for blk in range(2):
+                        nk = 2 * pos * (blk + 1)
+                        keys = kvv[slot, 0:nk, 0:HEAD]
+                        vals = kvv[slot, 0:nk, HEAD:2 * HEAD]
+                        q_all = jnp.concatenate([qv[slot, blk, :, hd * HEAD:(hd + 1) * HEAD] for hd in range(q_heads)], axis=0)
+                        sv[:, 0:nk] = lax.dot_general(q_all, keys, (((1,), (1,)), ((), ())), preferred_element_type=F32)
+                        for r0 in range(0, rows, SOFT):
+                            rs = slice(r0, r0 + SOFT)
+                            qpos = lax.broadcasted_iota(jnp.int32, (SOFT, 2 * pos), 0) + ((2 * blk + c) * pos + r0 % pos)
                             kpos = lax.broadcasted_iota(jnp.int32, (SOFT, 2 * pos), 1) + (nk - 2 * pos)
                             last = jnp.minimum(qpos, lv[a, pl.ds(b, 1), 0:2 * pos] - 1)
                             s = sv[rs, nk - 2 * pos:nk] * qscale
@@ -494,17 +531,114 @@
                                 s = jnp.concatenate([sv[rs, 0:2 * pos] * qscale, s], axis=1)
                             e = jnp.exp2(s - jnp.max(s, axis=-1, keepdims=True))
                             ov[0, rs, 0:nk] = (e / jnp.sum(e, axis=-1, keepdims=True)).astype(BF)
-                    for hd in range(q_heads):
-                        head(hd)
-                    o = jnp.dot(ov[0, :, 0:nk], vals, preferred_element_type=F32).astype(BF)
-                    for hd in range(q_heads):
-                        big[sh, row, hd * HEAD:(hd + 1) * HEAD] = o[hd * pos:(hd + 1) * pos]
-            loop(0, 2 * seqs, seq)
+                        o = jnp.dot(ov[0, :, 0:nk], vals, preferred_element_type=F32).astype(BF)
+                        per = TILE // HEAD
+                        for hd in range(q_heads):
+                            n = blk * n_q + hd // per
+                            ab[slot, n * pos:(n + 1) * pos, (hd % per) * HEAD:(hd % per + 1) * HEAD] = o[hd * pos:(hd + 1) * pos]
+                    for cp in o_stores(b, slot):
+                        cp.start()
+                loop(0, seqs, seq)
+                for b in (seqs - 2, seqs - 1):
+                    for cp in o_stores(b, b % 2):
+                        cp.wait()
+
+            def first_gu():
+                pl.when(l == 0)(lambda: arrive_gu(0))
+                load_gu(0, 1)
+            attend(0, first_gu)
+
+            early = early0 + (early1 - early0) * l
+
+            def gu_a(j):
+                slot = lax.rem(1 + j, 2)
+                s_lo = l * lax.max(1 - lax.div(j, n_own), 0)
+                wait_tile(slot)
+
+                def shard(s):
+                    @pl.when(jnp.logical_and(s == 1, j + 1 < early))
+                    def _():
+                        pl.when(jnp.logical_or(l == 0, j + 1 >= n_own))(lambda: arrive_gu(j + 1))
+                        load_gu(j + 1, 1 - slot)
+
+                    @pl.when(jnp.logical_and(s == 1, j + 1 == early))
+                    def _():
+                        load_kv(1)
+                    gu_step(s, j, slot, unless(jnp.logical_and(j == 0, s == s_lo), wait_half), s)
+                loop(s_lo, 3, shard)
+            loop(0, early, gu_a)
+
+            hf(l).wait_recv()
+            h_load(3).start()
+            load_q(0, 0)
+            wait_unit(1, 0)
+            h_load(3).wait()
+            kv_step(3, 1, wait_half, 3)
+
+            def q_b3(t):
+                slot = lax.rem(t, 2)
+
+                @pl.when(t + 1 < n_q)
+                def _():
+                    load_q(t + 1, 1 - slot)
+
+                @pl.when(t + 1 == n_q)
+                def _():
+                    load_gu(0, 1 - slot)
+                wait_tile(slot)
+                q_step(3, t, slot, either(t == 0, wait_half, wait_full), 2 + slot)
+
+                @pl.when(t == 0)
+                def _():
+                    kvx(l, 1).start()
+            loop(0, n_q, q_b3)
+
+            def gu_b(j):
+                slot = lax.rem(j, 2)
+
+                @pl.when(j + 1 < early)
+                def _():
+                    load_gu(j + 1, 1 - slot)
+
+                @pl.when(j + 1 == early)
+                def _():
+                    arrive_gu(early)
+                    load_gu(early, 1 - slot)
+                wait_tile(slot)
+                gu_step(3, j, slot, either(j == 0, wait_full, wait_half), 2 + slot)
+            loop(0, early, gu_b)
+            wait_half()
+            attend(1, nothing)
+
+            def gu_c(j):
+                slot = lax.rem(j, 2)
+                wait_tile(slot)
+
+                def shard(s):
+                    @pl.when(jnp.logical_and(s == 2, j + 1 < n_gu))
+                    def _():
+                        arrive_gu(j + 1)
+                        load_gu(j + 1, 1 - slot)
+
+                    @pl.when(jnp.logical_and(s == 2, j + 1 == n_gu))
+                    def _():
+                        load_o_near(l, 0, 1 - slot)
+                    gu_step(s, j, slot, unless(jnp.logical_and(j == early, s == 0), wait_half), s)
+                loop(0, 4, shard)
+            loop(early, n_gu, gu_c)
+            wait_half()
+            oslot = n_gu % 2
+
+            def om_load(s):
+                return (local(o_b.at[s], big.at[s, :, 0:aw], ol_s.at[s]), local(m_b.at[s], big.at[s, :, aw:kk], ml_s.at[s]))
+            for s in (2, 3, 1, 0):
+                for cp in om_load(s):
+                    cp.start()
 
             @pl.when(jnp.logical_and(giver, l == 0))
             def _():
-                loop(0, 2, lambda j: issue_gu(1, j))
-            loop(0, 4, lambda s: m_load(s).wait())
+                issue_kv(1)
+                issue_q(1, 0)
 
             def tau(k):
                 return lax.rem(y + lax.div(k, n_half), 2) * n_half + lax.rem(k, n_half)
@@ -547,7 +681,7 @@
 
                 @pl.when(jnp.logical_and(giver, jnp.logical_and(l == 0, jnp.logical_and(lax.rem(k, 2) == 1, k >= 3))))
                 def _():
-                    issue_gu(1, 2 + lax.div(k - 3, 2))
+                    issue_gu(1, lax.div(k - 3, 2))
 
             def out_tile(k):
                 slot = lax.rem(k + oslot, 2)
@@ -570,6 +704,10 @@
                         arrive_o(l, k + 1 - n_half)
                         load_o(l, r_at, r_ml, k + 1 - n_half, 1 - slot)
 
+                    @pl.when(k == 0)
+                    def _():
+                        for cp in om_load(s):
+                            cp.wait()
                     acc = jnp.dot(big[s], wv[slot], preferred_element_type=F32)
                     ov[s] = acc.astype(BF)
 
@@ -610,8 +748,7 @@
 
                 @pl.when(giver)
                 def _():
-                    loop(5, n_gu, lambda j: issue_gu(1, j))
-                    issue_qkv(1)
+                    loop(3, n_gu, lambda j: issue_gu(1, j))
                     loop(0, n_half, lambda t: issue_o(1, t))
 
             @pl.when(l == 1)
@@ -645,7 +782,8 @@
                 hx(l, b).wait_send()
             loop(0, n_hb, sent_h)
             hf(l).wait_send()
-            kvx(l).wait_send()
+            for a in range(2):
+                kvx(l, a).wait_send()
 
             def sent_z(t):
                 xz(l, t, 0).wait_send()
@@ -705,8 +843,9 @@
 
         outs = [buf(rows, d), buf(layers, dh, block_in), buf(layers, aw, dh), buf(layers, ff, dh),
                 buf(layers, dh, block_in), buf(layers, aw, dh), buf(layers, ff, dh),
-                buf(layers, 4, rows, d), buf(layers, 2, 4, rows, 2 * HEAD), buf(4, rows, aw), buf(4, rows, ff),
-                buf(layers, 4, rows, d), buf(layers, 2, rows, d), buf(layers, rows, d), buf(rows, d), buf(layers, rows, d), buf(rows, d)]
+                buf(layers, 4, rows, d), buf(layers, 2, 2, 2, rows, 2 * HEAD), buf(4, rows, aw), buf(4, rows, ff),
+                buf(layers, 4, rows, d), buf(layers, 2, rows, d), buf(layers, rows, d), buf(rows, d), buf(layers, rows, d), buf(rows, d),
+                buf(4, rows, aw)]
         dma = pltpu.SemaphoreType.DMA
         n_hb = rows // 128
         scratch = [pltpu.VMEM((4, rows, kk), BF), pltpu.VMEM((2, kk, TILE), BF), pltpu.VMEM((4, rows, TILE), BF),
@@ -719,11 +858,11 @@
                    dma((layers, n_out // 2, 2)), dma((layers, n_out // 2, 2)),
                    dma((layers, n_out // 2, 2)), dma((layers, n_out // 2, 2)),
                    dma((layers, n_hb)), dma((layers, n_hb)), dma((layers, n_hb)), dma((layers, n_hb)),
-                   dma((layers,)), dma((layers,)), dma((layers,)), dma((layers,)),
+                   dma((layers,)), dma((layers,)), dma((layers, 2)), dma((layers, 2)),
                    dma((layers, n_out, 2)), dma((layers, n_out, 2)), dma((layers, n_out)), dma((layers, n_out)),
                    dma((n_out,)), dma((n_out,)),
                    dma((2,)), dma((2,)), dma((2,)), dma((2, 4)), dma((2,)), dma((2,)), dma((4,)), dma((2, 4)), dma((4,)),
-                   dma((2, 6)), dma((4,)), dma((3,))]
+                   dma((2, 6)), dma((2, 2 * (aw // TILE))), dma((4,)), dma((4,)), dma((3,))]
         hbm = pl.BlockSpec(memory_space=pl.ANY)
         kernel = make_kernel(rows, seqs, d, dh, block_in, aw, ff, n_units)
         got = pl.pallas_call(

time: 1970 us -> 1950 us (0.990)
  Pallas kernels: 1950 us -> 1930 us
    pallas_call x1, Pallas kernels: 1950 us -> 1930 us  [device_step(): pl.pallas_call(kernel, out_shape=outs, in_specs=[hbm] * 6, out_specs=[hbm...]
where the time goes in v3:
time: 1950 us; the launch traced here: 1940 us
  Pallas kernels  1930 us (99%)
    pallas_call x1, Pallas kernels, device_step(): pl.pallas_call(kernel, out_shape=outs, in_specs=[hbm] * 6, out_specs=[hbm...  1930 us

profile of v3, /device:TPU:0, one launch (start us, length us, event | category | flops | bytes accessed | tf_op | source)
XLA Modules:
  0.0 1942.7 jit_solution(930842159834166143)
XLA Ops:
  0.0 1.3 broadcast_in_dim.4.lens
  1.3 1.4 broadcast_in_dim.5.gain
  2.7 1932.1 %two_layers.1 = (bf16[1024,4096]{1,0:T(8,128)(2,1)}, bf16[2,2048,8448]{2,1,0:T(8,128)(2,1)}, bf16[2,1024,2048]{2,1,0:T(8,128)(2,1)}, bf16[2,3584,2048]{2,1,0:T(8...) custom-call(bf16[1024,4096]{1,0:T(8,128)(2,1)} %bitcast.2, ...), custom_call_target="tpu_custom_call" | custom-call | tf_op jit(solution)/shard_map/two_layers/pallas_call | solution.py:868
  1934.8 7.9 copy.8

commit v4 on v3

--- a/solution.py
+++ b/solution.py
@@ -29,18 +29,19 @@
     pos = rows // seqs
     kk = aw + ff
     lnr = 64
-    early0, early1 = 6, 10
+    early0, late0, early1, late1 = 2, 6, 6, 10
     n_own = 2
     n_ln = rows // lnr
     n_hb = n_ln // 2
     hb = 2 * lnr
+    hr = rows // 2
     qscale = HEAD ** -0.5 * 1.4426950408889634
 
     def kernel(x, lens, gain, w_in, w_at, w_ml,
-               y_out, a_in, a_at, a_ml, r_in, r_at, r_ml, h_all, kvb, q_b, m_b, z_b, xr, sq, ym, yr, hid, o_b,
+               y_out, a_in, a_at, a_ml, r_in, r_at, r_ml, h_all, kvb, q_b, m_b, z_b, xr, sq, yr, hid, o_b,
                big, wv, ov, ab, xin, hst, gv, lv, qv, kvv, sv,
                a_s, a_r, wy_s, wy_r, wc_s, wc_r, oy_s, oy_r, oc_s, oc_r, hy_s, hy_r, hx_s, hx_r, hf_s, hf_r,
-               kv_s, kv_r, xz_s, xz_r, yz_s, yz_r, y3_s, y3_r, g_s, g_r, lg, li, lh, lo, hl, ws, os_, ai, ao, ml_s, ol_s, ad):
+               kv_s, kv_r, xz_s, xz_r, yz_s, yz_r, g_s, g_r, lg, li, lh, lo, hl, ws, os_, ai, ao, ml_s, ol_s, ad):
         rep = lax.axis_index('rep')
         y = lax.axis_index('data')
         m = lax.axis_index('model')
@@ -99,29 +100,20 @@
         def hx(l, b):
             return remote(h_all.at[l, 0, hrows(b)], h_all.at[l, 2, hrows(b)], hx_s.at[l, b], hx_r.at[l, b], xpeer)
 
-        def hf(l):
-            return remote(h_all.at[l, 1], h_all.at[l, 3], hf_s.at[l], hf_r.at[l], xpeer)
+        def hhalf(g):
+            return pl.ds(pl.multiple_of(g * hr, hr), hr)
+
+        def hf(l, g):
+            return remote(h_all.at[l, 1, hhalf(g)], h_all.at[l, 3, hhalf(g)], hf_s.at[l, g], hf_r.at[l, g], xpeer)
 
         def kvx(l, a):
             return remote(kvb.at[l, 0, a], kvb.at[l, 1, a], kv_s.at[l, a], kv_r.at[l, a], cpeer)
 
-        def xz(l, t, i):
-            return remote(z_b.at[l, 2 + i, :, tcols(t)], xr.at[l, i, :, tcols(t)], xz_s.at[l, t, i], xz_r.at[l, t, i], xpeer)
-
-        def yz(l, t):
-            return remote(sq.at[l, :, tcols(t)], yr.at[l, :, tcols(t)], yz_s.at[l, t], yz_r.at[l, t], ypeer)
-
-        def yz_first(l, t):
-            return remote(z_b.at[l, 1, :, tcols(t)], yr.at[l, :, tcols(t)], yz_s.at[l, t], yz_r.at[l, t], ypeer)
-
-        def yz_pass(l, t):
-            return remote(z_b.at[l, 3, :, tcols(t)], ym.at[:, tcols(t)], y3_s.at[t], y3_r.at[t], ypeer)
-
-        def xz_last(l, t):
-            return remote(sq.at[l, :, tcols(t)], xr.at[l, 0, :, tcols(t)], xz_s.at[l, t, 0], xz_r.at[l, t, 0], xpeer)
-
-        def y_goes_first(l, t):
-            return jnp.logical_and(l == 1, lax.rem(t, n_half) == n_half - 1)
+        def xz(l, w, i):
+            return remote(z_b.at[l, 2 + i, :, ucols(w)], xr.at[l, i, :, ucols(w)], xz_s.at[l, w, i], xz_r.at[l, w, i], xpeer)
+
+        def yz(l, w):
+            return remote(sq.at[l, :, ucols(w)], yr.at[l, :, ucols(w)], yz_s.at[l, w], yz_r.at[l, w], ypeer)
 
         def issue_gu(l, j):
             wy(l, gate_u + j).start()
@@ -158,9 +150,6 @@
             def _():
                 for fw in oc(l, t):
                     fw.wait_recv()
-
-        def near_in(l, u, slot, half):
-            return wv.at[slot, pl.ds(pl.multiple_of(y * dh, dh), dh), half * UNIT:(half + 1) * UNIT]
 
         def load_unit(l, u, slot, half):
             near = wv.at[slot, pl.ds(pl.multiple_of(y * dh, dh), dh), half * UNIT:(half + 1) * UNIT]
@@ -244,25 +233,23 @@
                         v = (v + (zs + xin[slot, 3, rs, :].astype(F32))).astype(BF)
                         hst[slot, rs, :] = v
                         v = v.astype(F32)
-                    if True:
-                        mean = jnp.sum(v, axis=-1, keepdims=True) * (1.0 / d)
-                        cen = v - mean
-                        var = jnp.sum(cen * cen, axis=-1, keepdims=True) * (1.0 / d)
-                        out = cen * lax.rsqrt(var + EPSILON) * gv[ln, 0:1, :]
-                        big[0, pl.ds(pl.multiple_of(r * lnr + i * 32, 32), 32), 0:d] = out.astype(BF)
+                    mean = jnp.sum(v, axis=-1, keepdims=True) * (1.0 / d)
+                    cen = v - mean
+                    var = jnp.sum(cen * cen, axis=-1, keepdims=True) * (1.0 / d)
+                    out = cen * lax.rsqrt(var + EPSILON) * gv[ln, 0:1, :]
+                    big[0, pl.ds(pl.multiple_of(r * lnr + i * 32, 32), 32), 0:d] = out.astype(BF)
                 loop(0, lnr // 32, sub)
                 if kind > 0:
                     store_o(r, slot).start()
-                if True:
-                    store_h(r, slot).start()
-
-                    @pl.when(r >= 1)
-                    def _():
-                        store_h(r - 1, 1 - slot).wait()
-
-                    @pl.when(jnp.logical_and(r >= 2, lax.rem(r, 2) == 0))
-                    def _():
-                        send(lax.div(r, 2) - 1)
+                store_h(r, slot).start()
+
+                @pl.when(r >= 1)
+                def _():
+                    store_h(r - 1, 1 - slot).wait()
+
+                @pl.when(jnp.logical_and(r >= 2, lax.rem(r, 2) == 0))
+                def _():
+                    send(lax.div(r, 2) - 1)
             loop(0, n_ln, block)
             if kind > 0:
                 store_o(n_ln - 2, 0).wait()
@@ -389,6 +376,26 @@
                     pl.when(jnp.logical_not(cond))(no)
                 return go
 
+            def quarter():
+                local(ov.at[0, 0:hr, 0:UNIT], m_b.at[0, 0:hr, ucols(0)], os_.at[0]).wait()
+
+            def m_part(g, j, buf):
+                return local(ov.at[buf, 0:hr, 0:UNIT], m_b.at[3, hhalf(g), ucols(j)], os_.at[0])
+
+            def q_part(g, t, buf):
+                return local(ov.at[buf, 0:hr], q_b.at[3, hhalf(g), tcols(t)], os_.at[0])
+
+            def kv_part(g, buf):
+                return local(ov.at[buf, 0:hr, 0:UNIT], kvb.at[l, 0, 1, 1, hhalf(g)], os_.at[0])
+
+            def gu_half(g, j, slot, before, buf):
+                acc = jnp.dot(big[3, hhalf(g), 0:d], wv[slot, 0:d, :], preferred_element_type=F32)
+                gg = acc[:, :UNIT].astype(BF).astype(F32)
+                u = acc[:, UNIT:].astype(BF).astype(F32)
+                ov[buf, 0:hr, 0:UNIT] = (gg * jax.nn.sigmoid(gg) * u).astype(BF)
+                before()
+                m_part(g, j, buf).start()
+
             def unless(cond, no):
                 return lambda: pl.when(jnp.logical_not(cond))(no)
 
@@ -436,7 +443,8 @@
                 load_kv(0)
 
             loop(0, n_hb, lambda b: hy(l, b).wait_recv())
-            hf(l).start()
+            for g in range(2):
+                hf(l, g).start()
             h_load(1).start()
             loop(0, n_hb, lambda b: hx(l, b).wait_recv())
             h_load(2).start()
@@ -549,89 +557,174 @@
             attend(0, first_gu)
 
             early = early0 + (early1 - early0) * l
-
-            def gu_a(j):
-                slot = lax.rem(1 + j, 2)
-                s_lo = l * lax.max(1 - lax.div(j, n_own), 0)
-                wait_tile(slot)
-
-                def shard(s):
-                    @pl.when(jnp.logical_and(s == 1, j + 1 < early))
-                    def _():
-                        pl.when(jnp.logical_or(l == 0, j + 1 >= n_own))(lambda: arrive_gu(j + 1))
+            late = late0 + (late1 - late0) * l
+
+            def part(g):
+                j_lo = early * g
+                j_hi = early + (late - early) * g
+
+                def gu_a(j):
+                    slot = lax.rem(1 + j + g, 2)
+                    s_lo = l * lax.max(1 - lax.div(j, n_own), 0)
+                    wait_tile(slot)
+
+                    def shard(s):
+                        @pl.when(jnp.logical_and(s == 1, j + 1 < j_hi))
+                        def _():
+                            pl.when(jnp.logical_or(l == 0, j + 1 >= n_own))(lambda: arrive_gu(j + 1))
+                            load_gu(j + 1, 1 - slot)
+
+                        @pl.when(jnp.logical_and(s == 1, j + 1 == j_hi))
+                        def _():
+                            load_kv(1 - g)
+
+                        def before():
+                            @pl.when(jnp.logical_and(s == s_lo, g == 1))
+                            def _():
+                                quarter()
+
+                            @pl.when(jnp.logical_or(s != s_lo, jnp.logical_and(g == 0, j != 0)))
+                            def _():
+                                wait_half()
+                        gu_step(s, j, slot, before, s)
+                    loop(s_lo, 3, shard)
+
+                    @pl.when(g == 1)
+                    def _():
+                        gu_half(0, j, slot, wait_half, 3)
+                loop(j_lo, j_hi, gu_a)
+
+                hf(l, g).wait_recv()
+                load = local(h_all.at[l, 3, hhalf(g)], big.at[3, hhalf(g), 0:d], hl.at[3])
+                load.start()
+                load_q(0, g)
+                wait_unit(1 - g, 0)
+                load.wait()
+                acc = jnp.dot(big[3, hhalf(g), 0:d], wv[1 - g, 0:d, 0:UNIT], preferred_element_type=F32)
+                ov[1, 0:hr, 0:UNIT] = acc.astype(BF)
+                either(g == 0, wait_half, quarter)()
+                kv_part(g, 1).start()
+
+                def q_b3(t):
+                    slot = lax.rem(t + g, 2)
+
+                    @pl.when(t + 1 < n_q)
+                    def _():
+                        load_q(t + 1, 1 - slot)
+
+                    @pl.when(t + 1 == n_q)
+                    def _():
+                        load_gu(0, 1 - slot)
+                    wait_tile(slot)
+                    buf = 3 - 2 * t
+                    ov[buf, 0:hr] = jnp.dot(big[3, hhalf(g), 0:d], wv[slot, 0:d, :], preferred_element_type=F32).astype(BF)
+                    either(t == 0, quarter, wait_half)()
+                    q_part(g, t, buf).start()
+
+                    @pl.when(jnp.logical_and(t == 0, g == 1))
+                    def _():
+                        kvx(l, 1).start()
+                loop(0, n_q, q_b3)
+
+                def gu_b(j):
+                    slot = lax.rem(j + g, 2)
+
+                    @pl.when(j + 1 < j_hi)
+                    def _():
                         load_gu(j + 1, 1 - slot)
 
-                    @pl.when(jnp.logical_and(s == 1, j + 1 == early))
-                    def _():
-                        load_kv(1)
-                    gu_step(s, j, slot, unless(jnp.logical_and(j == 0, s == s_lo), wait_half), s)
-                loop(s_lo, 3, shard)
-            loop(0, early, gu_a)
-
-            hf(l).wait_recv()
-            h_load(3).start()
-            load_q(0, 0)
-            wait_unit(1, 0)
-            h_load(3).wait()
-            kv_step(3, 1, wait_half, 3)
-
-            def q_b3(t):
-                slot = lax.rem(t, 2)
-
-                @pl.when(t + 1 < n_q)
-                def _():
-                    load_q(t + 1, 1 - slot)
-
-                @pl.when(t + 1 == n_q)
-                def _():
-                    load_gu(0, 1 - slot)
-                wait_tile(slot)
-                q_step(3, t, slot, either(t == 0, wait_half, wait_full), 2 + slot)
-
-                @pl.when(t == 0)
-                def _():
-                    kvx(l, 1).start()
-            loop(0, n_q, q_b3)
-
-            def gu_b(j):
-                slot = lax.rem(j, 2)
-
-                @pl.when(j + 1 < early)
-                def _():
-                    load_gu(j + 1, 1 - slot)
-
-                @pl.when(j + 1 == early)
-                def _():
-                    arrive_gu(early)
-                    load_gu(early, 1 - slot)
-                wait_tile(slot)
-                gu_step(3, j, slot, either(j == 0, wait_full, wait_half), 2 + slot)
-            loop(0, early, gu_b)
-            wait_half()
-            attend(1, nothing)
-
-            def gu_c(j):
-                slot = lax.rem(j, 2)
-                wait_tile(slot)
-
-                def shard(s):
-                    @pl.when(jnp.logical_and(s == 2, j + 1 < n_gu))
+                    @pl.when(j + 1 == j_hi)
+                    def _():
+                        arrive_gu(j_hi)
+                        load_gu(j_hi, 1 - slot)
+                    wait_tile(slot)
+                    gu_half(g, j, slot, either(j == 0, wait_half, quarter), 3 - 2 * lax.rem(j, 2))
+                loop(0, j_hi * g + early * (1 - g), gu_b)
+            loop(0, 2, part)
+            quarter()
+            def om_load(s):
+                return (local(o_b.at[s], big.at[s, :, 0:aw], ol_s.at[s]), local(m_b.at[s], big.at[s, :, aw:kk], ml_s.at[s]))
+            def tau(k):
+                return lax.rem(y + lax.div(k, n_half), 2) * n_half + lax.rem(k, n_half)
+
+            def z_store(s, t, buf):
+                return local(ov.at[buf], z_b.at[l, s, :, tcols(t)], os_.at[0])
+
+            def send_x(t, i):
+                for h in range(2):
+                    xz(l, 2 * t + h, i).start()
+
+            @pl.when(l == 1)
+            def _():
+                def ahead_gu(j):
+                    slot = lax.rem(1 + j, 2)
+
+                    @pl.when(j + 1 < n_gu)
                     def _():
                         arrive_gu(j + 1)
                         load_gu(j + 1, 1 - slot)
 
-                    @pl.when(jnp.logical_and(s == 2, j + 1 == n_gu))
+                    @pl.when(j + 1 == n_gu)
                     def _():
                         load_o_near(l, 0, 1 - slot)
-                    gu_step(s, j, slot, unless(jnp.logical_and(j == early, s == 0), wait_half), s)
-                loop(0, 4, shard)
-            loop(early, n_gu, gu_c)
+                    wait_tile(slot)
+                    gu_step(2, j, slot, unless(j == late, wait_half), slot)
+                loop(late, n_gu, ahead_gu)
+                wait_half()
+                for cp in om_load(2):
+                    cp.start()
+                for cp in om_load(2):
+                    cp.wait()
+
+                def ahead_out(k):
+                    slot = lax.rem(1 + k, 2)
+
+                    @pl.when(k + 1 < n_half)
+                    def _():
+                        load_o_near(l, k + 1, 1 - slot)
+
+                    @pl.when(k + 1 == n_half)
+                    def _():
+                        load_gu(late, 1 - slot)
+                    wait_o(slot)
+                    ov[slot] = jnp.dot(big[2], wv[slot], preferred_element_type=F32).astype(BF)
+
+                    @pl.when(k > 0)
+                    def _():
+                        z_store(2, 0, 0).wait()
+                        send_x(tau(k - 1), 0)
+                    z_store(2, tau(k), slot).start()
+                loop(0, n_half, ahead_out)
+                z_store(2, 0, 0).wait()
+                send_x(tau(n_half - 1), 0)
+            attend(1, nothing)
+
+            def gu_c(j):
+                slot = lax.rem(1 + j, 2)
+                wait_tile(slot)
+
+                def shard(i):
+                    s = i + l * lax.div(i, 2)
+
+                    @pl.when(jnp.logical_and(i == 1, j + 1 < n_gu))
+                    def _():
+                        pl.when(l == 0)(lambda: arrive_gu(j + 1))
+                        load_gu(j + 1, 1 - slot)
+
+                    @pl.when(jnp.logical_and(i == 1, j + 1 == n_gu))
+                    def _():
+                        load_o_near(l, 0, 1 - slot)
+                    gu_step(s, j, slot, unless(jnp.logical_and(j == late, i == 0), wait_half), s)
+                loop(0, 4 - l, shard)
+            loop(late, n_gu, gu_c)
             wait_half()
-            oslot = n_gu % 2
-
-            def om_load(s):
-                return (local(o_b.at[s], big.at[s, :, 0:aw], ol_s.at[s]), local(m_b.at[s], big.at[s, :, aw:kk], ml_s.at[s]))
-            for s in (2, 3, 1, 0):
+            oslot = (n_gu + 1) % 2
+
+            @pl.when(l == 0)
+            def _():
+                for cp in om_load(2):
+                    cp.start()
+            for s in (3, 1, 0):
                 for cp in om_load(s):
                     cp.start()
 
@@ -640,19 +733,15 @@
                 issue_kv(1)
                 issue_q(1, 0)
 
-            def tau(k):
-                return lax.rem(y + lax.div(k, n_half), 2) * n_half + lax.rem(k, n_half)
-
-            def z_store(s, t):
-                return local(ov.at[s], z_b.at[l, s, :, tcols(t)], os_.at[0])
-
             def add_tile(k):
                 t = tau(k)
-                first = y_goes_first(l, t)
-
-                def total(lhs_ref, rhs_ref):
-                    lhs = local(lhs_ref, ab.at[0], ad.at[0])
-                    rhs = local(rhs_ref, ab.at[1], ad.at[1])
+
+                def half(h):
+                    w = 2 * t + h
+                    xz(l, w, 0).wait_recv()
+                    xz(l, w, 1).wait_recv()
+                    lhs = local(z_b.at[l, 1, :, ucols(w)], ab.at[0, :, 0:UNIT], ad.at[0])
+                    rhs = local(xr.at[l, 1, :, ucols(w)], ab.at[1, :, 0:UNIT], ad.at[1])
                     lhs.start()
                     rhs.start()
                     lhs.wait()
@@ -660,33 +749,22 @@
 
                     def sub(i):
                         rs = pl.ds(pl.multiple_of(i * 128, 128), 128)
-                        ab[0, rs, :] = (ab[0, rs, :].astype(F32) + ab[1, rs, :].astype(F32)).astype(BF)
+                        ab[0, rs, 0:UNIT] = (ab[0, rs, 0:UNIT].astype(F32) + ab[1, rs, 0:UNIT].astype(F32)).astype(BF)
                     loop(0, rows // 128, sub)
-                    out = local(ab.at[0], sq.at[l, :, tcols(t)], ad.at[2])
+                    out = local(ab.at[0, :, 0:UNIT], sq.at[l, :, ucols(w)], ad.at[2])
                     out.start()
                     out.wait()
-
-                @pl.when(jnp.logical_not(first))
+                    yz(l, w).start()
+                loop(0, 2, half)
+
+                @pl.when(jnp.logical_and(jnp.logical_and(giver, l == 0), jnp.logical_or(k == 3, k == n_out - 1)))
                 def _():
-                    xz(l, t, 0).wait_recv()
-                    xz(l, t, 1).wait_recv()
-                    total(z_b.at[l, 1, :, tcols(t)], xr.at[l, 1, :, tcols(t)])
-                    yz(l, t).start()
-
-                @pl.when(first)
-                def _():
-                    yz_pass(l, t).wait_recv()
-                    total(z_b.at[l, 2, :, tcols(t)], ym.at[:, tcols(t)])
-                    xz_last(l, t).start()
-
-                @pl.when(jnp.logical_and(giver, jnp.logical_and(l == 0, jnp.logical_and(lax.rem(k, 2) == 1, k >= 3))))
-                def _():
-                    issue_gu(1, lax.div(k - 3, 2))
+                    issue_gu(1, lax.div(k, n_half))
 
             def out_tile(k):
                 slot = lax.rem(k + oslot, 2)
                 t = tau(k)
-                first = y_goes_first(l, t)
+                si_lo = l * (1 - lax.div(k, n_half))
                 wait_o(slot)
 
                 def order(si):
@@ -711,92 +789,79 @@
                     acc = jnp.dot(big[s], wv[slot], preferred_element_type=F32)
                     ov[s] = acc.astype(BF)
 
-                    @pl.when(jnp.logical_or(si > 0, k > 0))
-                    def _():
-                        z_store(0, t).wait()
-
-                    @pl.when(jnp.logical_and(jnp.logical_not(first), jnp.logical_and(si >= 1, si < 3)))
-                    def _():
-                        xz(l, t, si - 1).start()
-
-                    @pl.when(jnp.logical_and(first, si == 2))
-                    def _():
-                        yz_pass(l, t).start()
-
-                    @pl.when(jnp.logical_and(first, si == 3))
-                    def _():
-                        yz_first(l, t).start()
-                    z_store(s, t).start()
-                loop(0, 4, shard)
+                    @pl.when(jnp.logical_or(si > si_lo, k > 0))
+                    def _():
+                        z_store(0, t, 0).wait()
+
+                    @pl.when(jnp.logical_and(si >= 1 + si_lo, si < 3))
+                    def _():
+                        send_x(t, si - 1)
+                    z_store(s, t, s).start()
+                loop(si_lo, 4, shard)
 
                 @pl.when(jnp.logical_and(k >= 3, lax.rem(k, 2) == 1))
                 def _():
-                    add_tile(lax.div(k - 3, 2))
+                    done = lax.div(k - 3, 2) * (1 + l)
+                    loop(done, done + 1 + l, add_tile)
             loop(0, n_out, out_tile)
-            z_store(0, 0).wait()
-
-            loop(3, n_out, add_tile)
-
-            @pl.when(jnp.logical_and(giver, l == 0))
-            def _():
-                pass
-
+            z_store(0, 0, 0).wait()
+
+            def last_half(w):
+                yz(l, w).wait_recv()
+                parts = (hid.at[:, ucols(w)], z_b.at[l, 0, :, ucols(w)], xr.at[l, 0, :, ucols(w)], yr.at[l, :, ucols(w)])
+                cps = [local(p, ov.at[i, :, 0:UNIT], hl.at[i]) for i, p in enumerate(parts)]
+                for cp in cps:
+                    cp.start()
+                for cp in cps:
+                    cp.wait()
+
+                def sub(i):
+                    rs = pl.ds(pl.multiple_of(i * 128, 128), 128)
+                    zs = ov[1, rs, 0:UNIT].astype(F32) + ov[2, rs, 0:UNIT].astype(F32)
+                    ov[0, rs, 0:UNIT] = (ov[0, rs, 0:UNIT].astype(F32) + (zs + ov[3, rs, 0:UNIT].astype(F32))).astype(BF)
+                loop(0, rows // 128, sub)
+                out = local(ov.at[0, :, 0:UNIT], y_out.at[:, ucols(w)], lo.at[0])
+                out.start()
+                out.wait()
             @pl.when(l == 0)
             def _():
-                loop(0, n_out, lambda t: yz(l, t).wait_recv())
+                loop(3, n_out, add_tile)
+
+            @pl.when(l == 1)
+            def _():
+                def last_tile(k):
+                    loop(0, 2, lambda h: last_half(2 * tau(k) + h))
+                loop(0, 4, lambda i: last_tile(i + 2 * lax.div(i, 2)))
+                add_tile(6)
+                loop(0, 2, lambda i: last_tile(2 + 4 * i))
+                add_tile(7)
+                loop(0, 2, lambda i: last_tile(7 - 4 * i))
+
+            @pl.when(l == 0)
+            def _():
+                loop(0, 2 * n_out, lambda w: yz(l, w).wait_recv())
                 ln_phase(1)
 
                 @pl.when(giver)
                 def _():
-                    loop(3, n_gu, lambda j: issue_gu(1, j))
+                    loop(n_own, n_gu, lambda j: issue_gu(1, j))
                     loop(0, n_half, lambda t: issue_o(1, t))
 
-            @pl.when(l == 1)
-            def _():
-                def last_tile(k):
-                    t = lax.rem(1 - y + lax.div(k, n_half), 2) * n_half + lax.rem(k, n_half)
-
-                    @pl.when(y_goes_first(l, t))
-                    def _():
-                        xz(l, t, 0).wait_recv()
-                    yz(l, t).wait_recv()
-                    parts = (hid.at[:, tcols(t)], z_b.at[l, 0, :, tcols(t)], xr.at[l, 0, :, tcols(t)], yr.at[l, :, tcols(t)])
-                    cps = [local(p, ov.at[i], os_.at[i]) for i, p in enumerate(parts)]
-                    for cp in cps:
-                        cp.start()
-                    for cp in cps:
-                        cp.wait()
-
-                    def sub(i):
-                        rs = pl.ds(pl.multiple_of(i * 64, 64), 64)
-                        zs = ov[1, rs, :].astype(F32) + ov[2, rs, :].astype(F32)
-                        ov[0, rs, :] = (ov[0, rs, :].astype(F32) + (zs + ov[3, rs, :].astype(F32))).astype(BF)
-                    loop(0, rows // 64, sub)
-                    out = local(ov.at[0], y_out.at[:, tcols(t)], lo.at[0])
-                    out.start()
-                    out.wait()
-                loop(0, n_out, last_tile)
 
             def sent_h(b):
                 hy(l, b).wait_send()
                 hx(l, b).wait_send()
             loop(0, n_hb, sent_h)
-            hf(l).wait_send()
+            for g in range(2):
+                hf(l, g).wait_send()
             for a in range(2):
                 kvx(l, a).wait_send()
 
-            def sent_z(t):
-                xz(l, t, 0).wait_send()
-                yz(l, t).wait_send()
-
-                @pl.when(y_goes_first(l, t))
-                def _():
-                    yz_pass(l, t).wait_send()
-
-                @pl.when(jnp.logical_not(y_goes_first(l, t)))
-                def _():
-                    xz(l, t, 1).wait_send()
-            loop(0, n_out, sent_z)
+            def sent_z(w):
+                xz(l, w, 0).wait_send()
+                xz(l, w, 1).wait_send()
+                yz(l, w).wait_send()
+            loop(0, 2 * n_out, sent_z)
 
             @pl.when(giver)
             def _():
@@ -844,7 +909,7 @@
         outs = [buf(rows, d), buf(layers, dh, block_in), buf(layers, aw, dh), buf(layers, ff, dh),
                 buf(layers, dh, block_in), buf(layers, aw, dh), buf(layers, ff, dh),
                 buf(layers, 4, rows, d), buf(layers, 2, 2, 2, rows, 2 * HEAD), buf(4, rows, aw), buf(4, rows, ff),
-                buf(layers, 4, rows, d), buf(layers, 2, rows, d), buf(layers, rows, d), buf(rows, d), buf(layers, rows, d), buf(rows, d),
+                buf(layers, 4, rows, d), buf(layers, 2, rows, d), buf(layers, rows, d), buf(layers, rows, d), buf(rows, d),
                 buf(4, rows, aw)]
         dma = pltpu.SemaphoreType.DMA
         n_hb = rows // 128
@@ -858,9 +923,8 @@
                    dma((layers, n_out // 2, 2)), dma((layers, n_out // 2, 2)),
                    dma((layers, n_out // 2, 2)), dma((layers, n_out // 2, 2)),
                    dma((layers, n_hb)), dma((layers, n_hb)), dma((layers, n_hb)), dma((layers, n_hb)),
-                   dma((layers,)), dma((layers,)), dma((layers, 2)), dma((layers, 2)),
-                   dma((layers, n_out, 2)), dma((layers, n_out, 2)), dma((layers, n_out)), dma((layers, n_out)),
-                   dma((n_out,)), dma((n_out,)),
+                   dma((layers, 2)), dma((layers, 2)), dma((layers, 2)), dma((layers, 2)),
+                   dma((layers, 2 * n_out, 2)), dma((layers, 2 * n_out, 2)), dma((layers, 2 * n_out)), dma((layers, 2 * n_out)),
                    dma((2,)), dma((2,)), dma((2,)), dma((2, 4)), dma((2,)), dma((2,)), dma((4,)), dma((2, 4)), dma((4,)),
                    dma((2, 6)), dma((2, 2 * (aw // TILE))), dma((4,)), dma((4,)), dma((3,))]
         hbm = pl.BlockSpec(memory_space=pl.ANY)

time: 1950 us -> 1920 us (0.985)
  Pallas kernels: 1930 us -> 1910 us
    pallas_call x1, Pallas kernels: 1930 us -> 1910 us  [device_step(): pl.pallas_call(kernel, out_shape=outs, in_specs=[hbm] * 6, out_specs=[hbm...]
where the time goes in v4:
time: 1920 us
  Pallas kernels  1910 us (99%)
    pallas_call x1, Pallas kernels, device_step(): pl.pallas_call(kernel, out_shape=outs, in_specs=[hbm] * 6, out_specs=[hbm...  1910 us

profile of v4, /device:TPU:0, one launch (start us, length us, event | category | flops | bytes accessed | tf_op | source)
XLA Modules:
  0.0 1918.0 jit_solution(1587688433942464978)
XLA Ops:
  0.0 1.3 broadcast_in_dim.4.lens
  1.3 1.4 broadcast_in_dim.5.gain
  2.7 1907.4 %two_layers.1 = (bf16[1024,4096]{1,0:T(8,128)(2,1)}, bf16[2,2048,8448]{2,1,0:T(8,128)(2,1)}, bf16[2,1024,2048]{2,1,0:T(8,128)(2,1)}, bf16[2,3584,2048]{2,1,0:T(8...) custom-call(bf16[1024,4096]{1,0:T(8,128)(2,1)} %bitcast.2, ...), custom_call_target="tpu_custom_call" | custom-call | tf_op jit(solution)/shard_map/two_layers/pallas_call | solution.py:932
  1910.1 7.9 copy.8
